TPU v7x, 32 devices: a 4x2x2 block of a 4x4x8 slice. The times are simulated.
32 devices in a mesh: dp: 4 (over y, z), tp: 8 (over x, core).
Axes of the slice: x: 4, y: 2, z: 2, core: 2. Of those that a mesh axis runs over, the one named last changes fastest.
The devices are a block of a 4x4x8 slice.
Arguments:
- hidden: bfloat16 [4096, 1152], P('dp'), parts along dimension 0
- norm_gain: float32 [1152], replicated
- emb_table: bfloat16 [16384, 1152], P('tp')
- teacher_ids: int32 [4096, 256], P('dp'), parts along dimension 0
- teacher_q: float32 [4096, 256], P('dp'), parts along dimension 0
Outputs:
- output 1: float32 [4], P('dp'), parts along dimension 0
- output 2: bfloat16 [4096, 1152], P('dp'), parts along dimension 0
- output 3: float32 [4608], P('dp'), parts along dimension 0
- output 4: float32 [65536, 1152], P(('dp', 'tp')), parts along dimension 0
There are 4 independent parts. A program takes and returns all parts, laid end to end along the dimension named above; an argument that names none is the same for every part.
All inputs are finite; a program needn't handle non-finite values.
Results may differ from a plain program's by a relative error of at most 0.00161376.
Values sent between devices are 32-bit elements.
A program may use at most 768 MiB of HBM per device.

v0:
```python
import jax
import jax.numpy as jnp
from jax import lax
from jax.sharding import PartitionSpec as P


def norm_apply(hid_f, gain_vec):
    inv_rms = lax.rsqrt(jnp.mean(hid_f * hid_f, axis=-1, keepdims=True) + 1e-6)
    return hid_f * inv_rms * (1.0 + gain_vec)


def solution(mesh):
    def local_step(hidden, norm_gain, emb_block, teacher_ids, teacher_q):
        tokens = hidden.shape[0]
        block_rows = emb_block.shape[0]
        block_start = lax.axis_index('tp') * block_rows
        normed, norm_pull = jax.vjp(norm_apply, hidden.astype(jnp.float32), norm_gain)
        x_in = normed.astype(jnp.bfloat16)
        logits = lax.dot_general(x_in, emb_block, (((1,), (1,)), ((), ())), preferred_element_type=jnp.float32)
        row_peak = lax.pmax(jnp.max(logits, axis=1), 'tp')
        exp_total = lax.psum(jnp.sum(jnp.exp(logits - row_peak[:, None]), axis=1), 'tp')
        log_z = row_peak + jnp.log(exp_total)
        local_ids = teacher_ids - block_start
        is_owned = (local_ids >= 0) & (local_ids < block_rows)
        safe_ids = jnp.clip(local_ids, 0, block_rows - 1)
        picked_local = jnp.where(is_owned, jnp.take_along_axis(logits, safe_ids, axis=1), 0.0)
        picked = lax.psum(picked_local, 'tp')
        q_total = jnp.sum(teacher_q, axis=1)
        token_loss = q_total * log_z - jnp.sum(teacher_q * picked, axis=1)
        mean_loss = jnp.mean(token_loss)[None]
        softmax_p = jnp.exp(logits - log_z[:, None])
        row_index = jnp.arange(tokens)[:, None]
        target_q = jnp.zeros_like(logits).at[row_index, safe_ids].add(jnp.where(is_owned, teacher_q, 0.0))
        grad_z = ((softmax_p * q_total[:, None] - target_q) / tokens).astype(jnp.bfloat16)
        grad_part = jnp.dot(grad_z, emb_block, preferred_element_type=jnp.float32)
        grad_x = lax.psum(grad_part, 'tp')
        grad_block = lax.dot_general(grad_z, x_in, (((0,), (0,)), ((), ())), preferred_element_type=jnp.float32)
        grad_h, grad_gain = norm_pull(grad_x)
        return (mean_loss, grad_h.astype(jnp.bfloat16), grad_gain, grad_block)

    return jax.shard_map(local_step, mesh=mesh, in_specs=(P('dp', None), P(None), P('tp', None), P('dp', None), P('dp', None)), out_specs=(P('dp'), P('dp', None), P('dp'), P(('dp', 'tp'), None)), check_vma=False)
```

profile of v0, /device:TPU:81, one launch (start us, length us, event | category | flops | bytes accessed | tf_op | source)
XLA Modules:
  0.0 13959.8 jit_solution(7120124470383437030)
XLA Ops:
  7.2 0.1 all-reduce.3.cloned.1.call-start
  7.3 2.3 fusion.5
  9.6 0.7 broadcast_add_fusion
  10.3 2.8 or_bitcast_fusion
  13.2 0.5 copy.9
  13.8 8.6 fusion.17
  22.4 9148.0 %gather_fusion = f32[262144]{0:T(1024)} fusion(f32[1024,2048]{1,0:T(8,128)} %get-tuple-element.15, s32[262144]{0:T(1024)S(1)} %bitcast.18), kind=kCustom, calls=%fused_computation | custom fusion | bytes 4194304 | tf_op jit(solution)/shard_map/jit(take_along_axis)/gather | solution.py:26
  9170.4 2.6 reshape.50
  9173.0 3.1 select_bitcast_fusion.1
  9176.1 0.1 all-reduce.3.cloned.1.call-update
  9176.2 0.1 all-reduce.5.cloned.1.call-start
  9176.3 0.1 iota.3
  9176.4 0.4 and_reduce_fusion
  9176.8 0.2 multiply_reduce_fusion
  9177.1 0.1 select_bitcast_fusion
  9177.2 0.5 copy.10
  9177.7 0.5 copy.11
  9178.3 1399.6 %scatter_custom_fusion = f32[2097152]{0:T(1024)} fusion(s32[262144]{0:T(1024)S(1)} %bitcast.19, f32[262144]{0:T(1024)S(1)} %bitcast.20, f32[]{:T(128)} %constant.12.clone.1), kind=kCustom, calls=%fused_computation.16 | custom fusion | flops 262144 | bytes 8388612
  10577.9 9.3 reshape.46
  10587.2 3252.1 %pmax.7 = f32[1024]{0:T(1024)S(1)} all-reduce(f32[1024]{0:T(1024)S(1)} %copy-done.13), channel_id=1, replica_groups=mesh['dp'=4,'tp'=8] {'tp'}, use_global_device_ids=true, to_apply=%region_3.0 | all-reduce | flops 1024 | bytes 8192 | tf_op jit(solution)/shard_map/pmax | solution.py:20
  13839.3 4.6 exponential_reduce_fusion
  13843.9 15.6 psum.21
  13859.5 1.6 fusion.15
  13861.1 0.6 subtract_reduce_fusion
  13861.8 7.0 multiply_convert_fusion
  13868.8 2.1 copy-done.4
  13870.9 7.3 fusion.18
  13879.0 0.8 copy-done.1
  13879.9 9.9 fusion.10
  13889.7 55.2 all-reduce.5.cloned.1.call-done
  13944.9 4.6 fusion.3
  13949.5 2.3 fusion.4
  (41 shorter events, 0.2 us)
Async XLA Ops:
  7.2 6.6 copy-start
  7.2 13852.3 %all-reduce.3.cloned.1.call-start = ((), (), s32[]{:S(2)}) async-start(), calls=%async_computation | async-start | bytes 2097152 | tf_op jit(solution)/shard_map/psum | solution.py:27
  9.6 3.6 copy-start.11
  9.6 12.7 copy-start.9
  10.3 12.0 copy-start.7
  10.3 3.4 copy-start.16
  22.4 9150.6 %copy-start.5 = (s32[1024,256]{1,0:T(8,128)S(1)}, s32[1024,256]{1,0:T(8,128)}, u32[]{:S(2)}) copy-start(s32[1024,256]{1,0:T(8,128)} %param.8) | copy-start | bytes 3145732
  9170.4 6.0 copy-start.3
  9170.4 6.0 copy-start.14
  9173.0 3.8 copy-start.15
  9176.2 4768.7 %all-reduce.5.cloned.1.call-start = ((), (), s32[]{:S(2)}) async-start(), calls=%async_computation.1 | async-start | bytes 9437184 | tf_op jit(solution)/shard_map/psum | solution.py:36
  10577.9 9.3 copy-start.13
  10587.2 3272.3 %copy-start.6 = (f32[1024,256]{1,0:T(8,128)S(1)}, f32[1024,256]{1,0:T(8,128)}, u32[]{:S(2)}) copy-start(f32[1024,256]{1,0:T(8,128)} %param.9) | copy-start | bytes 3145732
  13859.5 11.4 slice-start
  13861.8 9.1 slice-start.1
  13868.8 2.1 copy-start.4
  13878.2 1.7 copy-start.1
  13878.2 1.7 copy-start.8
  13878.2 1.7 copy-start.10
  13889.7 59.7 copy-start.12
  13944.9 4.6 copy-start.2
Sparse Core Ops, SparseCore 0:
  9176.3 2942.6 all-reduce.2
  13878.4 66.4 all-reduce.4
where the time goes:
time: 14200 us; the launch traced here: 14000 us
  local copies, waits for them, and re-layouts  9160 us (65%)
  blocking collectives  3270 us (23%)
  other arithmetic  1430 us (10%)
    gather x3, local copies, waits for them, and re-layouts, local_step(): jnp.take_along_axis(logits, safe_ids, axis=1)  9150 us
    pmax x1, blocking collectives, local_step(): row_peak = lax.pmax(jnp.max(logits, axis=1), 'tp')  3250 us
    unnamed x7, other arithmetic  1410 us
  transfers between devices with their start and end apart: 2, of which 1 were waited for; matrix products, arithmetic and copies ran while one was open for 10% of the time, Pallas kernels for 0%

commit v1 on v0

v1 whole, which is shorter than its diff:
```python
import functools

import jax
import jax.numpy as jnp
from jax import lax
from jax.experimental import pallas as pl
from jax.experimental.pallas import tpu as pltpu
from jax.sharding import PartitionSpec as P

LANES = 128
TILE = 256


def norm_apply(hid_f, gain_vec):
    inv_rms = lax.rsqrt(jnp.mean(hid_f * hid_f, axis=-1, keepdims=True) + 1e-6)
    return hid_f * inv_rms * (1.0 + gain_vec)


def build_targets(lo_ref, hi_ref, qh_ref, qm_ref, ql_ref, dense_ref, tokens, groups):
    count = lo_ref.shape[1]
    sub = 16
    base = lax.broadcasted_iota(jnp.int32, (sub, count), 0).astype(jnp.float32).astype(jnp.bfloat16)
    zero = jnp.zeros((sub, count), jnp.bfloat16)
    one = jnp.ones((sub, count), jnp.bfloat16)

    def row(ref, n):
        return jnp.broadcast_to(ref[pl.ds(n, 1), :], (sub, count)).astype(jnp.bfloat16)

    def one_token(n):
        lo, hi = row(lo_ref, n), row(hi_ref, n)
        low_hot = jnp.concatenate([jnp.where(lo == base + jnp.bfloat16(sub * k), one, zero) for k in range(LANES // sub)], axis=0)
        pieces = []
        for ref in (qh_ref, qm_ref, ql_ref):
            q = row(ref, n)
            for k in range(groups // sub):
                pieces.append(jnp.where(hi == base + jnp.bfloat16(sub * k), q, zero))
        lhs = jnp.concatenate(pieces, axis=0)
        out = lax.dot_general(lhs, low_hot, (((1,), (1,)), ((), ())), preferred_element_type=jnp.float32)
        total = out[:groups] + out[groups:2 * groups] + out[2 * groups:]
        dense_ref[pl.ds(n, groups, stride=tokens), :] = total

    unroll = 8

    @pl.loop(0, tokens // unroll)
    def _(i):
        for u in range(unroll):
            one_token(i * unroll + u)


def dz_kernel(scale, z_ref, lid_ref, q_ref, lz_ref, dz_ref, loss_ref, lo_s, hi_s, qh_s, qm_s, ql_s, dense_s):
    tokens, vocab = z_ref.shape
    groups = vocab // LANES
    lid = lid_ref[...]
    lo_s[...] = jnp.bitwise_and(lid, LANES - 1).astype(jnp.float32)
    hi_s[...] = jnp.right_shift(lid, 7).astype(jnp.float32)
    q = q_ref[...]
    qh = q.astype(jnp.bfloat16).astype(jnp.float32)
    rest = q - qh
    qm = rest.astype(jnp.bfloat16).astype(jnp.float32)
    qh_s[...] = qh
    qm_s[...] = qm
    ql_s[...] = rest - qm
    build_targets(lo_s, hi_s, qh_s, qm_s, ql_s, dense_s, tokens, groups)
    total = jnp.sum(q, axis=1, keepdims=True)
    part = jnp.zeros((8, LANES), jnp.float32)
    for r in range(0, tokens, LANES):
        rows = pl.ds(r, LANES)
        lz = lz_ref[rows, :]
        s = jnp.broadcast_to(total[r:r + LANES], (LANES, LANES))
        for g in range(groups):
            cols = pl.ds(g * LANES, LANES)
            z = z_ref[rows, cols]
            target = dense_s[pl.ds(g * tokens + r, LANES), :]
            dz_ref[rows, cols] = ((jnp.exp(z - lz) * s - target) * scale).astype(jnp.bfloat16)
            part += jnp.sum((target * z).reshape(LANES // 8, 8, LANES), axis=0)
    loss_ref[...] = part


def solution(mesh):
    def local_step(hidden, norm_gain, emb_block, teacher_ids, teacher_q):
        tokens = hidden.shape[0]
        vocab = emb_block.shape[0]
        count = teacher_ids.shape[1]
        block_start = lax.axis_index('tp') * vocab
        normed, norm_pull = jax.vjp(norm_apply, hidden.astype(jnp.float32), norm_gain)
        x_in = normed.astype(jnp.bfloat16)
        logits = lax.dot_general(x_in, emb_block, (((1,), (1,)), ((), ())), preferred_element_type=jnp.float32)
        row_peak = lax.pmax(jnp.max(logits, axis=1), 'tp')
        exp_total = lax.psum(jnp.sum(jnp.exp(logits - row_peak[:, None]), axis=1), 'tp')
        log_z = row_peak + jnp.log(exp_total)
        tile = min(TILE, tokens)
        steps = tokens // tile
        spec = lambda width: pl.BlockSpec((tile, width), lambda i: (i, 0))
        grad_z, loss_part = pl.pallas_call(
            functools.partial(dz_kernel, 1.0 / tokens),
            grid=(steps,),
            out_shape=(jax.ShapeDtypeStruct((tokens, vocab), jnp.bfloat16), jax.ShapeDtypeStruct((8 * steps, LANES), jnp.float32)),
            in_specs=[spec(vocab), spec(count), spec(count), spec(LANES)],
            out_specs=(spec(vocab), pl.BlockSpec((8, LANES), lambda i: (i, 0))),
            scratch_shapes=[pltpu.VMEM((tile, count), jnp.float32)] * 5 + [pltpu.VMEM((tile * vocab // LANES, LANES), jnp.float32)],
            compiler_params=pltpu.CompilerParams(vmem_limit_bytes=48 * 2**20),
            cost_estimate=pl.CostEstimate(flops=2 * 48 * 256 * 128 * tokens, bytes_accessed=12 * tokens * vocab // 2, transcendentals=tokens * vocab),
        )(logits, teacher_ids - block_start, teacher_q, jnp.broadcast_to(log_z[:, None], (tokens, LANES)))
        picked = lax.psum(jnp.sum(loss_part), 'tp')
        mean_loss = ((jnp.sum(jnp.sum(teacher_q, axis=1) * log_z) - picked) / tokens)[None]
        grad_part = jnp.dot(grad_z, emb_block, preferred_element_type=jnp.float32)
        grad_x = lax.psum(grad_part, 'tp')
        grad_block = lax.dot_general(grad_z, x_in, (((0,), (0,)), ((), ())), preferred_element_type=jnp.float32)
        grad_h, grad_gain = norm_pull(grad_x)
        return (mean_loss, grad_h.astype(jnp.bfloat16), grad_gain, grad_block)

    return jax.shard_map(local_step, mesh=mesh, in_specs=(P('dp', None), P(None), P('tp', None), P('dp', None), P('dp', None)), out_specs=(P('dp'), P('dp', None), P('dp'), P(('dp', 'tp'), None)), check_vma=False)
```

time: 14200 us -> 192 us (0.01); the launches traced: 14000 us -> 191 us
  local copies, waits for them, and re-layouts: 9160 us -> 0.22 us
  blocking collectives: 3270 us -> 41.9 us
  other arithmetic: 1430 us -> 16 us
    gather x3 -> x0, local copies, waits for them, and re-layouts: 9150 us -> none  [local_step(): jnp.take_along_axis(logits, safe_ids, axis=1)]
    pmax x1, blocking collectives: 3250 us -> 14 us  [local_step(): row_peak = lax.pmax(jnp.max(logits, axis=1), 'tp')]
    unnamed x7 -> x1, other arithmetic: 1410 us -> 0.01 us
  transfers between devices with their start and end apart: 2 -> 1, of which waited for: 1 -> 1; matrix products, arithmetic and copies ran while one was open for 10% -> 5% of each run, Pallas kernels for 0% -> 0%
where the time goes in v1:
time: 192 us; the launch traced here: 191 us
  Pallas kernels  45.2 us (24%)
  blocking collectives  41.9 us (22%)
  waiting for transfers between devices  41.9 us (22%)
  matrix products  29.6 us (15%)
  between operations  16.6 us (9%)
  other arithmetic  16 us (8%)
    pallas_call x1, Pallas kernels, local_step(): pl.pallas_call(functools.partial(dz_kernel, 1.0 / tokens), grid=(steps,),...  45.2 us
    psum x1, waiting for transfers between devices, local_step(): grad_x = lax.psum(grad_part, 'tp')  41.9 us
    psum x1, blocking collectives, local_step(): lax.psum(jnp.sum(jnp.exp(logits - row_peak[:, None]), axis=1), 'tp')  14.5 us
    pmax x1, blocking collectives, local_step(): row_peak = lax.pmax(jnp.max(logits, axis=1), 'tp')  14 us
    psum x1, blocking collectives, local_step(): picked = lax.psum(jnp.sum(loss_part), 'tp')  13.4 us
    dot_general x1, matrix products, local_step(): lax.dot_general(x_in, emb_block, (((1,), (1,)), ((), ())), preferred_elem...  10.9 us
    dot_general x1, matrix products, local_step(): lax.dot_general(grad_z, x_in, (((0,), (0,)), ((), ())), preferred_element...  9.9 us
    dot_general x1, matrix products, local_step(): grad_part = jnp.dot(grad_z, emb_block, preferred_element_type=jnp.float32)  8.81 us
  transfers between devices with their start and end apart: 1, of which 1 were waited for; matrix products, arithmetic and copies ran while one was open for 5% of the time, Pallas kernels for 0%

profile of v1, /device:TPU:81, one launch (start us, length us, event | category | flops | bytes accessed | tf_op | source)
XLA Modules:
  0.0 191.5 jit_solution(7023457300142929308)
XLA Ops:
  7.2 0.1 all-reduce.2.cloned.1.call-start
  7.2 2.2 %fusion.5 = f32[1024]{0:T(1024)S(1)} fusion(bf16[1024,1152]{1,0:T(8,128)(2,1)} %param.5), kind=kLoop, calls=%fused_computation.11 | loop fusion | flops 3537920 | bytes 2363392 | tf_op jit(solution)/shard_map/jvp()/reduce_sum | solution.py:15
  9.5 0.7 broadcast_add_fusion
  10.2 10.9 %fusion.12 = (f32[1024]{0:T(1024)S(1)}, f32[1024,2048]{1,0:T(8,128)}) fusion(bf16[2048,1152]{1,0:T(8,128)(2,1)} %param.7, bf16[1024,1152]{1,0:T(8,128)(2,1)} %param.5, f32[1152]{0:T(1024)S(1)} %broadcast_add_fusion, f32[1024]{0:T(1024)S(1)} %fusion.11), kind=kOutput, calls=%fused_computation.22 | convolution fusion | flops 4838652928 | bytes 15479296 | tf_op jit(solution)/shard_map/dot_general | solution.py:87
  21.1 0.0 copy-start
  21.1 14.0 %pmax.7 = f32[1024]{0:T(1024)S(1)} all-reduce(f32[1024]{0:T(1024)S(1)} %get-tuple-element.12), channel_id=1, replica_groups=mesh['dp'=4,'tp'=8] {'tp'}, use_global_device_ids=true, to_apply=%region_3.0 | all-reduce | flops 1024 | bytes 8192 | tf_op jit(solution)/shard_map/pmax | solution.py:88
  35.0 0.0 copy-start.3
  35.0 4.7 %exponential_reduce_fusion = f32[1024]{0:T(1024)S(1)} fusion(f32[1024,2048]{1,0:T(8,128)} %get-tuple-element.13.z_ref, f32[1024]{0:T(1024)S(1)} %pmax.7), kind=kLoop, calls=%fused_computation | loop fusion | flops 4193280 | bytes 8396800 | tf_op jit(solution)/shard_map/reduce_sum | solution.py:89
  39.7 14.5 %psum.21 = f32[1024]{0:T(1024)S(1)} all-reduce(f32[1024]{0:T(1024)S(1)} %exponential_reduce_fusion), channel_id=1, replica_groups=mesh['dp'=4,'tp'=8] {'tp'}, use_global_device_ids=true, to_apply=%region_5.0 | all-reduce | flops 1024 | bytes 8192 | tf_op jit(solution)/shard_map/psum | solution.py:89
  54.3 0.0 copy-done
  54.3 0.2 reduce_sum.62
  54.5 0.0 copy-done.3
  54.5 0.0 slice-start
  54.5 0.1 broadcast_subtract_fusion.lid_ref
  54.6 0.6 multiply_reduce_fusion
  55.2 0.2 broadcast_in_dim.6.lz_ref
  55.4 0.0 slice-start.1
  55.4 45.2 %shard_map.84 = (bf16[1024,2048]{1,0:T(8,128)(2,1)}, f32[32,128]{1,0:T(8,128)S(1)}) custom-call(f32[1024,2048]{1,0:T(8,128)} %get-tuple-element.13.z_ref, s32[1024,256]{1,0:T(8,128)S(1)} %broadcast_subtract_fusion.lid_ref, f32[1024,256]{1,0:T(8,128)S(1)} %copy-done, f32[1024,128]{1,0:T(8,128)S(1)} %broadcast_in_dim.6.lz_ref), custom_call_target="tpu_custom_call" | custom-call | flops 3221225472 | bytes 12582912 | tf_op jit(solution)/shard_map/pallas_call | solution.py:94
  100.7 0.0 slice-done
  100.7 0.0 slice-done.1
  100.7 8.8 %fusion.13 = f32[1024,1152]{1,0:T(8,128)} fusion(bf16[1024,2048]{1,0:T(8,128)(2,1)} %get-tuple-element.7, bf16[2048,1152]{1,0:T(8,128)(2,1)S(1)} %bitcast.6), kind=kOutput, calls=%fused_computation.23 | convolution fusion | flops 4831838208 | bytes 13631488 | tf_op jit(solution)/shard_map/dot_general | solution.py:106
  109.5 0.0 copy-start.1
  109.5 0.1 all-reduce.2.cloned.1.call-update
  109.5 0.6 reduce_sum.75
  110.1 13.4 %psum.22 = f32[]{:T(128)} all-reduce(f32[]{:T(128)} %reduce_sum.75), channel_id=1, replica_groups=mesh['dp'=4,'tp'=8] {'tp'}, use_global_device_ids=true, to_apply=%region_8.0 | all-reduce | flops 1 | bytes 8 | tf_op jit(solution)/shard_map/psum | solution.py:104
  124.8 0.0 copy-done.1
  124.8 9.9 %fusion.7 = f32[2048,1152]{1,0:T(8,128)} fusion(bf16[1024,2048]{1,0:T(8,128)(2,1)} %get-tuple-element.7, bf16[1024,1152]{1,0:T(8,128)(2,1)S(1)} %copy-done.1, f32[1152]{0:T(1024)S(1)} %broadcast_add_fusion, f32[1024]{0:T(1024)S(1)} %fusion.11), kind=kOutput, calls=%fused_computation.13 | convolution fusion | flops 4836556800 | bytes 15999488 | tf_op jit(solution)/shard_map/dot_general | solution.py:108
  134.7 41.9 %all-reduce.2.cloned.1.call-done = f32[1024,1152]{1,0:T(8,128)} async-done(((f32[1024,1152]{1,0:T(8,128)}), f32[1024,1152]{1,0:T(8,128)}) %all-reduce.2.cloned.1.call-update) | async-done | bytes 4718608 | tf_op jit(solution)/shard_map/psum | solution.py:107
  176.6 0.0 copy-start.2
  176.6 4.6 %fusion.3 = (f32[1152]{0:T(1024)}, f32[1024]{0:T(1024)S(1)}) fusion(f32[1024,1152]{1,0:T(8,128)} %all-reduce.2.cloned.1.call-done, bf16[1024,1152]{1,0:T(8,128)(2,1)S(1)} %copy-done.1, f32[1024]{0:T(1024)S(1)} %fusion.11, f32[1152]{0:T(1024)S(1)} %broadcast_add_fusion), kind=kLoop, calls=%fused_computation.9 | loop fusion | flops 8255360 | bytes 7095296 | tf_op jit(solution)/shard_map/transpose(jvp())/reduce_sum | solution.py:16
  181.2 0.0 copy-done.2
  181.2 2.3 %fusion.4 = bf16[1024,1152]{1,0:T(8,128)(2,1)} fusion(bf16[1024,1152]{1,0:T(8,128)(2,1)S(1)} %copy-done.1, f32[1024,1152]{1,0:T(8,128)S(1)} %copy-done.2, f32[1024]{0:T(1024)S(1)} %multiply_multiply_fusion, f32[1152]{0:T(1024)S(1)} %broadcast_add_fusion, f32[1024]{0:T(1024)S(1)} %fusion.11), kind=kLoop, calls=%fused_computation.10 | loop fusion | flops 8257536 | bytes 9449984 | tf_op jit(solution)/shard_map/convert_element_type | solution.py:110
  (3 shorter events, 0.0 us)
Async XLA Ops:
  7.2 169.4 %all-reduce.2.cloned.1.call-start = ((), (), s32[]{:S(2)}) async-start(), calls=%async_computation | async-start | bytes 9437184 | tf_op jit(solution)/shard_map/psum | solution.py:107
  21.1 33.2 %copy-start = (f32[1024,256]{1,0:T(8,128)S(1)}, f32[1024,256]{1,0:T(8,128)}, u32[]{:S(2)}) copy-start(f32[1024,256]{1,0:T(8,128)} %q_ref.1) | copy-start | bytes 3145732
  35.0 19.5 %copy-start.3 = (s32[1024,256]{1,0:T(8,128)S(1)}, s32[1024,256]{1,0:T(8,128)}, u32[]{:S(2)}) copy-start(s32[1024,256]{1,0:T(8,128)} %param.8) | copy-start | bytes 3145732
  54.5 46.2 %slice-start = ((s8[4718592]{0:T(1024)(128)(4,1)}), s8[4194304]{0:T(1024)(128)(4,1)S(1)}, s32[]{:S(2)}) async-start(s8[4718592]{0:T(1024)(128)(4,1)} %bitcast.5), calls=%async_computation.1 | async-start | bytes 8388608
  55.4 45.3 %slice-start.1 = ((s8[4718592]{0:T(1024)(128)(4,1)}), s8[524288]{0:T(1024)(128)(4,1)S(1)}, s32[]{:S(2)}) async-start(s8[4718592]{0:T(1024)(128)(4,1)} %bitcast.5), calls=%async_computation.2 | async-start | bytes 1048576
  109.5 15.3 %copy-start.1 = (bf16[1024,1152]{1,0:T(8,128)(2,1)S(1)}, bf16[1024,1152]{1,0:T(8,128)(2,1)}, u32[]{:S(2)}) copy-start(bf16[1024,1152]{1,0:T(8,128)(2,1)} %param.5) | copy-start | bytes 7077892
  176.6 4.6 %copy-start.2 = (f32[1024,1152]{1,0:T(8,128)S(1)}, f32[1024,1152]{1,0:T(8,128)}, u32[]{:S(2)}) copy-start(f32[1024,1152]{1,0:T(8,128)} %all-reduce.2.cloned.1.call-done) | copy-start | bytes 14155780
Sparse Core Ops, SparseCore 0:
  109.7 66.8 all-reduce.1

commit v2 on v0

v2 whole, which is shorter than its diff:
```python
import functools

import jax
import jax.numpy as jnp
from jax import lax
from jax.experimental import pallas as pl
from jax.experimental.pallas import tpu as pltpu
from jax.sharding import PartitionSpec as P

LANES = 128
CHUNK = 128
BLOCK = 256
UNROLL = 16
MESH = pl.DeviceIdType.MESH
LAG_A, LAG_B, LAG_C, LAG_D, LAG_E, LAG_F = 1, 2, 3, 4, 5, 6
(K_SIB, K_FAR_R, K_FAR_L, K_NEAR_R, K_NEAR_L, K_SUM_R, K_SUM_L, K_OUT_R, K_OUT_L, K_OUT_S,
 K_PASS_R, K_PASS_L, K_FWD_L, K_FWD_R, K_FWD_O) = range(15)
KINDS = 15


def build_targets(lo_ref, code_ref, pieces, dense_ref, tokens, groups):
    count = lo_ref.shape[1]
    sub, half = 16, LANES // 2
    base = lax.broadcasted_iota(jnp.int32, (sub, count), 0).astype(jnp.float32).astype(jnp.bfloat16)
    zero = jnp.zeros((sub, count), jnp.bfloat16)
    one = jnp.ones((sub, count), jnp.bfloat16)

    def row(ref, n):
        return jnp.broadcast_to(ref[pl.ds(n, 1), :], (sub, count)).astype(jnp.bfloat16)

    def one_token(n):
        lo, code = row(lo_ref, n), row(code_ref, n)
        weights = [row(ref, n) for ref in pieces]
        low_hot = jnp.concatenate([jnp.where(lo == base + jnp.bfloat16(sub * k), one, zero) for k in range(half // sub)], axis=0)
        here = [code == base + jnp.bfloat16(sub * k) for k in range(2 * groups // sub)]
        lhs = jnp.concatenate([jnp.where(h, w, zero) for w in weights for h in here], axis=0)
        out = lax.dot_general(lhs, low_hot, (((1,), (1,)), ((), ())), preferred_element_type=jnp.float32)
        out = out[:2 * groups] + out[2 * groups:4 * groups] + out[4 * groups:]
        dense_ref[pl.ds(n * (groups + 1), groups), :] = jnp.concatenate([out[:groups], out[groups:]], axis=1)

    @pl.loop(0, tokens // UNROLL)
    def _(i):
        for u in range(UNROLL):
            one_token(i * UNROLL + u)


def kernel(n_tp, hid_hbm, gain_ref, emb_hbm, ids_hbm, q_hbm, dh_hbm, x_hbm, dz_hbm, fin_ref,
           hid, emb, ids, q, xs, z, dz, lz_s, lo_s, code_s, qh_s, qm_s, ql_s, dense, part, sib_buf, ring_buf,
           grad, dh_s, dw_acc, loss_acc, slz_acc, stat_buf, fin_buf,
           in_sem, emb_sem, out_sem, dh_sem, x_sem, stat_send, stat_recv, fin_send, fin_recv, send_sem, recv_sem):
    tokens, width = hid.shape
    vocab = emb.shape[0]
    groups = vocab // LANES
    chunks = tokens // CHUNK
    chips = n_tp // 2
    half = CHUNK // 2
    own = half // chips
    bit = own // 2
    scale = 1.0 / tokens
    dp, me = lax.axis_index('dp'), lax.axis_index('tp')
    core = lax.rem(me, 2)
    chip = me // 2
    right = lax.rem(chip + 1, chips)
    left = lax.rem(chip + chips - 1, chips)
    far = lax.rem(chip + 2, chips)
    to_right, to_left, to_sib = right * 2 + core, left * 2 + core, chip * 2 + 1 - core

    barrier = pltpu.get_barrier_semaphore()
    for d in range(1, n_tp):
        pl.semaphore_signal(barrier, inc=1, device_id=(dp, lax.rem(me + d, n_tp)), device_id_type=MESH)

    get_hid = pltpu.make_async_copy(hid_hbm, hid, in_sem.at[0])
    get_ids = pltpu.make_async_copy(ids_hbm, ids, in_sem.at[1])
    get_q = pltpu.make_async_copy(q_hbm, q, in_sem.at[2])

    def get_emb(b):
        rows = pl.ds(pl.multiple_of(b * BLOCK, BLOCK), BLOCK)
        return pltpu.make_async_copy(emb_hbm.at[rows], emb.at[rows], emb_sem.at[b])

    get_hid.start()
    for b in range(vocab // BLOCK):
        get_emb(b).start()
    get_ids.start()
    get_q.start()

    get_hid.wait()
    gain = 1.0 + gain_ref[...]

    @pl.loop(0, tokens // 32)
    def _(i):
        rows = pl.ds(pl.multiple_of(i * 32, 32), 32)
        h = hid[rows, :].astype(jnp.float32)
        inv = lax.rsqrt(jnp.mean(h * h, axis=1, keepdims=True) + 1e-6)
        xs[rows, :] = (h * inv * gain).astype(jnp.bfloat16)

    put_x = pltpu.make_async_copy(xs, x_hbm, x_sem)
    put_x.start()

    @pl.loop(0, vocab // BLOCK)
    def _(b):
        get_emb(b).wait()
        rows = pl.ds(pl.multiple_of(b * BLOCK, BLOCK), BLOCK)
        for r in range(0, tokens, min(512, tokens)):
            z[b, pl.ds(r, min(512, tokens)), :] = lax.dot_general(xs[pl.ds(r, min(512, tokens)), :], emb[rows, :], (((1,), (1,)), ((), ())), preferred_element_type=jnp.float32)

    eye = lax.broadcasted_iota(jnp.int32, (LANES, LANES), 0) == lax.broadcasted_iota(jnp.int32, (LANES, LANES), 1)

    def as_row(tile):
        return jnp.sum(jnp.where(eye, tile, 0.0), axis=0, keepdims=True)

    stat_rows = tokens // LANES

    @pl.loop(0, stat_rows)
    def _(t):
        for u in range(0, LANES, 32):
            rows = pl.ds(pl.multiple_of(t * LANES + u, 32), 32)
            tiles = [z[g // 2, rows, pl.ds((g % 2) * LANES, LANES)] for g in range(groups)]
            peak = functools.reduce(jnp.maximum, tiles)
            peak = jnp.broadcast_to(jnp.max(peak, axis=1, keepdims=True), (32, LANES))
            total = functools.reduce(jnp.add, [jnp.exp(v - peak) for v in tiles])
            lz_s[rows, :] = peak
            dense[pl.ds(u, 32), :] = jnp.broadcast_to(jnp.sum(total, axis=1, keepdims=True), (32, LANES))
        stat_buf[me, pl.ds(t, 1), :] = as_row(lz_s[pl.ds(pl.multiple_of(t * LANES, LANES), LANES), :])
        stat_buf[me, pl.ds(stat_rows + t, 1), :] = as_row(dense[pl.ds(0, LANES), :])

    def everyone(buf, send, recv, d):
        return pltpu.make_async_remote_copy(
            src_ref=buf.at[me], dst_ref=buf.at[me], send_sem=send.at[d - 1], recv_sem=recv.at[d - 1],
            device_id=(dp, lax.rem(me + d, n_tp)), device_id_type=MESH)

    pl.semaphore_wait(barrier, n_tp - 1)
    for d in range(1, n_tp):
        everyone(stat_buf, stat_send, stat_recv, d).start()

    get_ids.wait()
    get_q.wait()
    start = me * vocab

    def prepare(c):
        @pl.loop(0, CHUNK // 32)
        def _(i):
            rows = pl.ds(pl.multiple_of(i * 32, 32), 32)
            src = pl.ds(pl.multiple_of(c * CHUNK + i * 32, 32), 32)
            lid = ids[src, :] - start
            lo_s[rows, :] = jnp.bitwise_and(lid, LANES // 2 - 1).astype(jnp.float32)
            code = jnp.right_shift(lid, 7) + groups * jnp.bitwise_and(jnp.right_shift(lid, 6), 1)
            code_s[rows, :] = jnp.where((lid >= 0) & (lid < vocab), code, -1).astype(jnp.float32)
            w = q[src, :] * scale
            wh = w.astype(jnp.bfloat16).astype(jnp.float32)
            rest = w - wh
            wm = rest.astype(jnp.bfloat16).astype(jnp.float32)
            qh_s[rows, :] = wh
            qm_s[rows, :] = wm
            ql_s[rows, :] = rest - wm

    prepare(0)
    build_targets(lo_s, code_s, (qh_s, qm_s, ql_s), dense, CHUNK, groups)

    for d in range(1, n_tp):
        everyone(stat_buf, stat_send, stat_recv, d).wait_recv()
    peaks = [stat_buf[k, pl.ds(0, stat_rows), :] for k in range(n_tp)]
    peak = functools.reduce(jnp.maximum, peaks)
    total = functools.reduce(jnp.add, [stat_buf[k, pl.ds(stat_rows, stat_rows), :] * jnp.exp(peaks[k] - peak) for k in range(n_tp)])
    log_z = peak + jnp.log(total)
    for t in range(stat_rows):
        tile = jnp.where(eye, jnp.broadcast_to(log_z[t:t + 1, :], (LANES, LANES)), 0.0)
        lz_s[pl.ds(t * LANES, LANES), :] = jnp.broadcast_to(jnp.sum(tile, axis=1, keepdims=True), (LANES, LANES))

    fin_buf[me] = jnp.zeros(fin_buf.shape[1:], jnp.float32)
    dw_acc[...] = jnp.zeros_like(dw_acc)
    loss_acc[...] = jnp.zeros_like(loss_acc)
    slz_acc[...] = jnp.zeros_like(slz_acc)

    mine = core * half
    theirs = half - mine

    def at(base, block, off=0):
        return base + block * own + off

    def rdma(c, kind):
        def rows(first, count):
            return pl.ds(pl.multiple_of(first, 8), count)

        if kind == K_SIB:
            src, dst, peer = part.at[c, rows(theirs, half)], sib_buf.at[c], to_sib
        elif kind in (K_FAR_R, K_FAR_L, K_NEAR_R, K_NEAR_L, K_SUM_R, K_SUM_L):
            first = {K_FAR_R: at(mine, far), K_FAR_L: at(mine, far, bit), K_NEAR_R: at(mine, right, bit),
                     K_NEAR_L: at(mine, left), K_SUM_R: at(mine, right), K_SUM_L: at(mine, left, bit)}[kind]
            src, dst = part.at[c, rows(first, bit)], ring_buf.at[c, kind - K_FAR_R]
            peer = to_right if kind in (K_FAR_R, K_NEAR_R, K_SUM_R) else to_left
        else:
            first, count, peer = {
                K_OUT_R: (at(mine, chip), own, to_right), K_OUT_L: (at(mine, chip), own, to_left), K_OUT_S: (at(mine, chip), own, to_sib),
                K_PASS_R: (at(mine, left), bit, to_right), K_PASS_L: (at(mine, right, bit), bit, to_left),
                K_FWD_L: (at(mine, left), own, to_sib), K_FWD_R: (at(mine, right), own, to_sib), K_FWD_O: (at(mine, far), own, to_sib)}[kind]
            src = dst = grad.at[c, rows(first, count)]
        return pltpu.make_async_remote_copy(src_ref=src, dst_ref=dst, send_sem=send_sem.at[c, kind], recv_sem=recv_sem.at[c, kind],
                                            device_id=(dp, peer), device_id_type=MESH)

    def put_dz(c):
        rows = pl.ds(pl.multiple_of(c * CHUNK, CHUNK), CHUNK)
        return pltpu.make_async_copy(dz.at[rows], dz_hbm.at[rows], out_sem.at[c])

    def put_dh(c):
        rows = pl.ds(pl.multiple_of(c * CHUNK, CHUNK), CHUNK)
        return pltpu.make_async_copy(dh_s.at[rows], dh_hbm.at[rows], dh_sem.at[c])

    def compute(c):
        sub = 32
        first = pl.multiple_of(c * CHUNK, CHUNK)

        @pl.loop(0, CHUNK // sub)
        def _(i):
            r = pl.multiple_of(i * sub, sub)
            rows = pl.ds(pl.multiple_of(first + r, sub), sub)
            lz = lz_s[rows, :]
            s = jnp.broadcast_to(jnp.sum(q[rows, :], axis=1, keepdims=True) * scale, (sub, LANES))
            acc = jnp.zeros((8, LANES), jnp.float32)
            for g in range(groups):
                v = z[g // 2, rows, pl.ds((g % 2) * LANES, LANES)]
                target = dense[pl.ds(r * (groups + 1) + g, sub, stride=groups + 1), :]
                dz[rows, pl.ds(g * LANES, LANES)] = (jnp.exp(v - lz) * s - target).astype(jnp.bfloat16)
                acc += jnp.sum((target * v).reshape(sub // 8, 8, LANES), axis=0)
            loss_acc[...] += acc
            slz_acc[...] += jnp.sum((s * lz).reshape(sub // 8, 8, LANES), axis=0)

        put_dz(c).start()
        part[c] = jnp.dot(dz[pl.ds(first, CHUNK), :], emb[...], preferred_element_type=jnp.float32)
        rdma(c, K_SIB).start()

        @pl.when(c < chunks - 1)
        def _():
            prepare(c + 1)
            build_targets(lo_s, code_s, (qh_s, qm_s, ql_s), dense, CHUNK, groups)

    def part_rows(first, count):
        return pl.ds(pl.multiple_of(first, 8), count)

    def stage_a(c):
        rdma(c, K_SIB).wait_recv()
        rows = part_rows(mine, half)
        part[c, rows, :] += sib_buf[c]
        for kind in (K_FAR_R, K_FAR_L, K_NEAR_R, K_NEAR_L):
            rdma(c, kind).start()

    def stage_b(c):
        rdma(c, K_FAR_R).wait_recv()
        part[c, part_rows(at(mine, right), bit), :] += ring_buf[c, 0]
        rdma(c, K_SUM_R).start()
        rdma(c, K_FAR_L).wait_recv()
        part[c, part_rows(at(mine, left, bit), bit), :] += ring_buf[c, 1]
        rdma(c, K_SUM_L).start()

    def stage_c(c):
        for kind in (K_NEAR_R, K_NEAR_L, K_SUM_R, K_SUM_L):
            rdma(c, kind).wait_recv()
        dx = part[c, part_rows(at(mine, chip), own), :] + jnp.concatenate(
            [ring_buf[c, K_SUM_R - 1] + ring_buf[c, K_NEAR_L - 1], ring_buf[c, K_SUM_L - 1] + ring_buf[c, K_NEAR_R - 1]], axis=0)
        h = hid[pl.ds(pl.multiple_of(c * CHUNK + at(mine, chip), own), own), :].astype(jnp.float32)
        inv = lax.rsqrt(jnp.mean(h * h, axis=1, keepdims=True) + 1e-6)
        unit = h * inv
        dy = dx * gain
        grad[c, part_rows(at(mine, chip), own), :] = inv * (dy - unit * jnp.mean(dy * unit, axis=1, keepdims=True))
        dw_acc[...] += jnp.sum((dx * unit).reshape(own // 8, 8, width), axis=0)
        for kind in (K_OUT_R, K_OUT_L, K_OUT_S):
            rdma(c, kind).start()

        @pl.when(c == chunks - 1)
        def _():
            dw = jnp.sum(dw_acc[...], axis=0, keepdims=True)
            for i in range(width // LANES):
                fin_buf[me, pl.ds(i, 1), :] = dw[:, i * LANES:(i + 1) * LANES]
            fin_buf[me, pl.ds(width // LANES, 1), :] = jnp.sum(loss_acc[...], axis=0, keepdims=True)
            for d in range(1, n_tp):
                everyone(fin_buf, fin_send, fin_recv, d).start()

    def stage_d(c):
        rdma(c, K_OUT_R).wait_recv()
        rdma(c, K_PASS_R).start()
        rdma(c, K_FWD_L).start()
        rdma(c, K_OUT_L).wait_recv()
        rdma(c, K_PASS_L).start()
        rdma(c, K_FWD_R).start()

    def stage_e(c):
        rdma(c, K_PASS_R).wait_recv()
        rdma(c, K_PASS_L).wait_recv()
        rdma(c, K_FWD_O).start()

    def stage_f(c):
        for kind in (K_OUT_S, K_FWD_L, K_FWD_R, K_FWD_O):
            rdma(c, kind).wait_recv()
        dh_s[pl.ds(pl.multiple_of(c * CHUNK, CHUNK), CHUNK), :] = grad[c].astype(jnp.bfloat16)
        put_dh(c).start()

    stages = ((LAG_F, stage_f), (LAG_E, stage_e), (LAG_D, stage_d), (LAG_C, stage_c), (LAG_B, stage_b), (LAG_A, stage_a), (0, compute))

    @pl.loop(0, chunks + LAG_F)
    def _(step):
        for lag, stage in stages:
            c = step - lag

            @pl.when((c >= 0) & (c < chunks))
            def _(c=c, stage=stage):
                stage(c)

    for d in range(1, n_tp):
        everyone(fin_buf, fin_send, fin_recv, d).wait_recv()
    fin = functools.reduce(jnp.add, [fin_buf[k] for k in range(n_tp)])
    lanes = width // LANES
    loss = jnp.sum(slz_acc[:, 0:1], axis=0, keepdims=True) - jnp.sum(fin[lanes:lanes + 1, :], axis=1, keepdims=True)
    fin_ref[...] = fin
    fin_ref[pl.ds(lanes, 1), :] = jnp.broadcast_to(loss, (1, LANES))

    for d in range(1, n_tp):
        everyone(stat_buf, stat_send, stat_recv, d).wait_send()
        everyone(fin_buf, fin_send, fin_recv, d).wait_send()

    @pl.loop(0, chunks)
    def _(c):
        for kind in range(KINDS):
            rdma(c, kind).wait_send()
        put_dz(c).wait()
        put_dh(c).wait()

    put_x.wait()


def solution(mesh):
    n_tp = mesh.shape['tp']

    def local_step(hidden, norm_gain, emb_block, teacher_ids, teacher_q):
        tokens, width = hidden.shape
        vocab = emb_block.shape[0]
        count = teacher_ids.shape[1]
        chunks = tokens // CHUNK
        half = CHUNK // 2
        bit = half // (n_tp // 2) // 2
        f32, bf16 = jnp.float32, jnp.bfloat16
        dma = pltpu.SemaphoreType.DMA
        hbm, vmem = pl.BlockSpec(memory_space=pl.ANY), pl.BlockSpec(memory_space=pltpu.VMEM)
        dh, x_in, grad_z, fin = pl.pallas_call(
            functools.partial(kernel, n_tp),
            out_shape=(jax.ShapeDtypeStruct((tokens, width), bf16), jax.ShapeDtypeStruct((tokens, width), bf16),
                       jax.ShapeDtypeStruct((tokens, vocab), bf16), jax.ShapeDtypeStruct((16, LANES), f32)),
            in_specs=[hbm, vmem, hbm, hbm, hbm],
            out_specs=(hbm, hbm, hbm, vmem),
            scratch_shapes=[
                pltpu.VMEM((tokens, width), bf16), pltpu.VMEM((vocab, width), bf16), pltpu.VMEM((tokens, count), jnp.int32), pltpu.VMEM((tokens, count), f32),
                pltpu.VMEM((tokens, width), bf16), pltpu.VMEM((vocab // BLOCK, tokens, BLOCK), f32), pltpu.VMEM((tokens, vocab), bf16), pltpu.VMEM((tokens, LANES), f32),
                *[pltpu.VMEM((CHUNK, count), f32)] * 5, pltpu.VMEM((CHUNK * (vocab // LANES + 1), LANES), f32),
                pltpu.VMEM((chunks, CHUNK, width), f32), pltpu.VMEM((chunks, half, width), f32), pltpu.VMEM((chunks, 6, bit, width), f32),
                pltpu.VMEM((chunks, CHUNK, width), f32), pltpu.VMEM((tokens, width), bf16),
                pltpu.VMEM((8, width), f32), pltpu.VMEM((8, LANES), f32), pltpu.VMEM((8, LANES), f32),
                pltpu.VMEM((n_tp, 2 * tokens // LANES, LANES), f32), pltpu.VMEM((n_tp, 16, LANES), f32),
                dma((3,)), dma((vocab // BLOCK,)), dma((chunks,)), dma((chunks,)), dma(()),
                dma((n_tp - 1,)), dma((n_tp - 1,)), dma((n_tp - 1,)), dma((n_tp - 1,)), dma((chunks, KINDS)), dma((chunks, KINDS)),
            ],
            compiler_params=pltpu.CompilerParams(collective_id=0, has_side_effects=True, vmem_limit_bytes=60 * 2**20),
        )(hidden, norm_gain[None, :], emb_block, teacher_ids, teacher_q)
        grad_block = lax.dot_general(grad_z, x_in, (((0,), (0,)), ((), ())), preferred_element_type=f32)
        lanes = width // LANES
        return fin[lanes, :1], dh, fin[:lanes].reshape(-1), grad_block

    return jax.shard_map(local_step, mesh=mesh, in_specs=(P('dp', None), P(None), P('tp', None), P('dp', None), P('dp', None)), out_specs=(P('dp'), P('dp', None), P('dp'), P(('dp', 'tp'), None)), check_vma=False)
```

time: 14200 us -> 104 us (0.01); the launches traced: 14000 us -> 104 us
  local copies, waits for them, and re-layouts: 9160 us -> 3.82 us
  blocking collectives: 3270 us -> 0 us
  other arithmetic: 1430 us -> 0 us
    gather x3 -> x0, local copies, waits for them, and re-layouts: 9150 us -> none  [local_step(): jnp.take_along_axis(logits, safe_ids, axis=1)]
    pmax x1 -> x0, blocking collectives: 3250 us -> none  [local_step(): row_peak = lax.pmax(jnp.max(logits, axis=1), 'tp')]
    unnamed x7 -> x0, other arithmetic: 1410 us -> none
  transfers between devices with their start and end apart: 2 -> 0, of which waited for: 1 -> 0; matrix products, arithmetic and copies ran while one was open for 10% -> 0% of each run, Pallas kernels for 0% -> 0%
where the time goes in v2:
time: 104 us
  Pallas kernels  89.3 us (86%)
  matrix products  10.5 us (10%)
  local copies, waits for them, and re-layouts  3.82 us (4%)
    pallas_call x1, Pallas kernels, local_step(): pl.pallas_call(functools.partial(kernel, n_tp), out_shape=(jax.ShapeDtype...  89.3 us
    dot_general x1, matrix products, local_step(): lax.dot_general(grad_z, x_in, (((0,), (0,)), ((), ())), preferred_element...  10.5 us

profile of v2, /device:TPU:81, one launch (start us, length us, event | category | flops | bytes accessed | tf_op | source)
XLA Modules:
  0.0 104.3 jit_solution(7343289198968241897)
XLA Ops:
  0.6 1.3 %broadcast_in_dim.3.gain_ref = f32[1,1152]{1,0:T(1,128)} reshape(f32[1152]{0:T(1024)} %param.6) | data formatting | bytes 9216 | tf_op jit(solution)/shard_map/broadcast_in_dim | solution.py:360
  1.9 89.3 %shard_map.84 = (bf16[1024,1152]{1,0:T(8,128)(2,1)}, bf16[1024,1152]{1,0:T(8,128)(2,1)}, bf16[1024,2048]{1,0:T(8,128)(2,1)}, f32[16,128]{1,0:T(8,128)}) custom-call(bf16[1024,1152]{1,0:T(8,128)(2,1)} %hid_hbm.1, f32[1,1152]{1,0:T(1,128)} %broadcast_in_dim.3.gain_ref, bf16[2048,1152]{1,0:T(8,128)(2,1)} %emb_hbm.1, s32[1024,256]{1,0:T(8,128)} %ids_hbm.1, ...), custom_call_target="tpu_custom_call" | custom-call | tf_op jit(solution)/shard_map/pallas_call | solution.py:342
  91.2 0.0 copy-start.1
  91.2 0.0 copy-start
  91.2 10.5 %fusion = f32[2048,1152]{1,0:T(8,128)} fusion(bf16[1024,2048]{1,0:T(8,128)(2,1)} %get-tuple-element.10, bf16[1024,1152]{1,0:T(8,128)(2,1)} %get-tuple-element.11), kind=kOutput, calls=%fused_computation.1 | convolution fusion | flops 4831838208 | bytes 15990784 | tf_op jit(solution)/shard_map/dot_general | solution.py:361
  101.7 0.0 copy-done.1
  101.7 0.6 slice_bitcast_fusion
  102.3 0.5 slice.6
  102.9 0.0 copy-done
  102.9 1.4 %copy.10 = bf16[1024,1152]{1,0:T(8,128)(2,1)} copy(bf16[1024,1152]{1,0:T(8,128)(2,1)S(1)} %copy-done) | data formatting | bytes 4718592
Async XLA Ops:
  91.2 10.5 %copy-start.1 = (f32[16,128]{1,0:T(8,128)S(1)}, f32[16,128]{1,0:T(8,128)}, u32[]{:S(2)}) copy-start(f32[16,128]{1,0:T(8,128)} %get-tuple-element.8) | copy-start | bytes 24580
  91.2 11.7 %copy-start = (bf16[1024,1152]{1,0:T(8,128)(2,1)S(1)}, bf16[1024,1152]{1,0:T(8,128)(2,1)}, u32[]{:S(2)}) copy-start(bf16[1024,1152]{1,0:T(8,128)(2,1)} %get-tuple-element.17) | copy-start | bytes 7077892

commit v3 on v2

--- a/solution.py
+++ b/solution.py
@@ -10,15 +10,16 @@
 LANES = 128
 CHUNK = 128
 BLOCK = 256
-UNROLL = 16
+UNROLL = 32
 MESH = pl.DeviceIdType.MESH
-LAG_A, LAG_B, LAG_C, LAG_D, LAG_E, LAG_F = 1, 2, 3, 4, 5, 6
+SLOTS = 3
+LAG_A, LAG_B, LAG_C, LAG_D, LAG_E, LAG_F = 2, 6, 10, 14, 17, 18
 (K_SIB, K_FAR_R, K_FAR_L, K_NEAR_R, K_NEAR_L, K_SUM_R, K_SUM_L, K_OUT_R, K_OUT_L, K_OUT_S,
  K_PASS_R, K_PASS_L, K_FWD_L, K_FWD_R, K_FWD_O) = range(15)
 KINDS = 15
 
 
-def build_targets(lo_ref, code_ref, pieces, dense_ref, tokens, groups):
+def build_targets(lo_ref, code_ref, pieces, dense_ref, first, tokens, groups):
     count = lo_ref.shape[1]
     sub, half = 16, LANES // 2
     base = lax.broadcasted_iota(jnp.int32, (sub, count), 0).astype(jnp.float32).astype(jnp.bfloat16)
@@ -41,7 +42,7 @@
     @pl.loop(0, tokens // UNROLL)
     def _(i):
         for u in range(UNROLL):
-            one_token(i * UNROLL + u)
+            one_token(first + i * UNROLL + u)
 
 
 def kernel(n_tp, hid_hbm, gain_ref, emb_hbm, ids_hbm, q_hbm, dh_hbm, x_hbm, dz_hbm, fin_ref,
@@ -84,7 +85,7 @@
     get_q.start()
 
     get_hid.wait()
-    gain = 1.0 + gain_ref[...]
+    gain = 1.0 + gain_ref[...].reshape(1, width)
 
     @pl.loop(0, tokens // 32)
     def _(i):
@@ -154,7 +155,7 @@
             ql_s[rows, :] = rest - wm
 
     prepare(0)
-    build_targets(lo_s, code_s, (qh_s, qm_s, ql_s), dense, CHUNK, groups)
+    build_targets(lo_s, code_s, (qh_s, qm_s, ql_s), dense, 0, CHUNK, groups)
 
     for d in range(1, n_tp):
         everyone(stat_buf, stat_send, stat_recv, d).wait_recv()
@@ -228,11 +229,6 @@
         part[c] = jnp.dot(dz[pl.ds(first, CHUNK), :], emb[...], preferred_element_type=jnp.float32)
         rdma(c, K_SIB).start()
 
-        @pl.when(c < chunks - 1)
-        def _():
-            prepare(c + 1)
-            build_targets(lo_s, code_s, (qh_s, qm_s, ql_s), dense, CHUNK, groups)
-
     def part_rows(first, count):
         return pl.ds(pl.multiple_of(first, 8), count)
 
@@ -295,14 +291,25 @@
 
     stages = ((LAG_F, stage_f), (LAG_E, stage_e), (LAG_D, stage_d), (LAG_C, stage_c), (LAG_B, stage_b), (LAG_A, stage_a), (0, compute))
 
-    @pl.loop(0, chunks + LAG_F)
-    def _(step):
+    @pl.loop(0, SLOTS * chunks + LAG_F - SLOTS + 1)
+    def _(slot):
         for lag, stage in stages:
-            c = step - lag
-
-            @pl.when((c >= 0) & (c < chunks))
-            def _(c=c, stage=stage):
-                stage(c)
+            since = slot - lag
+
+            @pl.when((since >= 0) & (lax.rem(since + SLOTS * LAG_F, SLOTS) == 0) & (since < SLOTS * chunks))
+            def _(since=since, stage=stage):
+                stage(since // SLOTS)
+
+        phase = lax.rem(slot, SLOTS)
+        c = slot // SLOTS
+
+        @pl.when((phase == 1) & (c < chunks - 1))
+        def _():
+            prepare(c + 1)
+
+        @pl.when((phase >= 1) & (c < chunks - 1))
+        def _():
+            build_targets(lo_s, code_s, (qh_s, qm_s, ql_s), dense, (phase - 1) * (CHUNK // 2), CHUNK // 2, groups)
 
     for d in range(1, n_tp):
         everyone(fin_buf, fin_send, fin_recv, d).wait_recv()
@@ -357,7 +364,7 @@
                 dma((n_tp - 1,)), dma((n_tp - 1,)), dma((n_tp - 1,)), dma((n_tp - 1,)), dma((chunks, KINDS)), dma((chunks, KINDS)),
             ],
             compiler_params=pltpu.CompilerParams(collective_id=0, has_side_effects=True, vmem_limit_bytes=60 * 2**20),
-        )(hidden, norm_gain[None, :], emb_block, teacher_ids, teacher_q)
+        )(hidden, norm_gain, emb_block, teacher_ids, teacher_q)
         grad_block = lax.dot_general(grad_z, x_in, (((0,), (0,)), ((), ())), preferred_element_type=f32)
         lanes = width // LANES
         return fin[lanes, :1], dh, fin[:lanes].reshape(-1), grad_block

time: 104 us -> 97.4 us (0.937)
  Pallas kernels: 89.3 us -> 83.6 us
  local copies, waits for them, and re-layouts: 3.82 us -> 2.53 us
    pallas_call x1, Pallas kernels: 89.3 us -> 83.6 us  [local_step(): pl.pallas_call(functools.partial(kernel, n_tp), out_shape=(jax.ShapeDtype...]
    broadcast_in_dim x1 -> x0, local copies, waits for them, and re-layouts: 1.29 us -> none  [local_step(): norm_gain[None, :]]
where the time goes in v3:
time: 97.4 us; the launch traced here: 97.3 us
  Pallas kernels  83.6 us (86%)
  matrix products  10.5 us (11%)
  local copies, waits for them, and re-layouts  2.53 us (3%)
    pallas_call x1, Pallas kernels, local_step(): pl.pallas_call(functools.partial(kernel, n_tp), out_shape=(jax.ShapeDtype...  83.6 us
    dot_general x1, matrix products, local_step(): lax.dot_general(grad_z, x_in, (((0,), (0,)), ((), ())), preferred_element...  10.5 us

profile of v3, /device:TPU:81, one launch (start us, length us, event | category | flops | bytes accessed | tf_op | source)
XLA Modules:
  0.0 97.3 jit_solution(5920348825959841451)
XLA Ops:
  0.6 83.6 %shard_map.84 = (bf16[1024,1152]{1,0:T(8,128)(2,1)}, bf16[1024,1152]{1,0:T(8,128)(2,1)}, bf16[1024,2048]{1,0:T(8,128)(2,1)}, f32[16,128]{1,0:T(8,128)}) custom-call(bf16[1024,1152]{1,0:T(8,128)(2,1)} %hid_hbm.1, f32[1152]{0:T(1024)} %gain_ref.1, bf16[2048,1152]{1,0:T(8,128)(2,1)} %emb_hbm.1, s32[1024,256]{1,0:T(8,128)} %ids_hbm.1, f32[1024,256]{1,0:T(8,128)} %q_hbm.1), custom_call_target="tpu_custom_call" | custom-call | tf_op jit(solution)/shard_map/pallas_call | solution.py:349
  84.2 0.0 copy-start.1
  84.2 0.0 copy-start
  84.3 10.5 %fusion = f32[2048,1152]{1,0:T(8,128)} fusion(bf16[1024,2048]{1,0:T(8,128)(2,1)} %get-tuple-element.10, bf16[1024,1152]{1,0:T(8,128)(2,1)} %get-tuple-element.11), kind=kOutput, calls=%fused_computation.1 | convolution fusion | flops 4831838208 | bytes 15990784 | tf_op jit(solution)/shard_map/dot_general | solution.py:368
  94.8 0.0 copy-done.1
  94.8 0.6 slice_bitcast_fusion
  95.4 0.5 slice.6
  95.9 0.0 copy-done
  95.9 1.4 %copy.10 = bf16[1024,1152]{1,0:T(8,128)(2,1)} copy(bf16[1024,1152]{1,0:T(8,128)(2,1)S(1)} %copy-done) | data formatting | bytes 4718592
Async XLA Ops:
  84.2 10.5 %copy-start.1 = (f32[16,128]{1,0:T(8,128)S(1)}, f32[16,128]{1,0:T(8,128)}, u32[]{:S(2)}) copy-start(f32[16,128]{1,0:T(8,128)} %get-tuple-element.8) | copy-start | bytes 24580
  84.2 11.7 %copy-start = (bf16[1024,1152]{1,0:T(8,128)(2,1)S(1)}, bf16[1024,1152]{1,0:T(8,128)(2,1)}, u32[]{:S(2)}) copy-start(bf16[1024,1152]{1,0:T(8,128)(2,1)} %get-tuple-element.17) | copy-start | bytes 7077892

commit v4 on v3

--- a/solution.py
+++ b/solution.py
@@ -10,7 +10,7 @@
 LANES = 128
 CHUNK = 128
 BLOCK = 256
-UNROLL = 32
+SUB = 32
 MESH = pl.DeviceIdType.MESH
 SLOTS = 3
 LAG_A, LAG_B, LAG_C, LAG_D, LAG_E, LAG_F = 2, 6, 10, 14, 17, 18
@@ -39,16 +39,14 @@
         out = out[:2 * groups] + out[2 * groups:4 * groups] + out[4 * groups:]
         dense_ref[pl.ds(n * (groups + 1), groups), :] = jnp.concatenate([out[:groups], out[groups:]], axis=1)
 
-    @pl.loop(0, tokens // UNROLL)
-    def _(i):
-        for u in range(UNROLL):
-            one_token(first + i * UNROLL + u)
-
-
-def kernel(n_tp, hid_hbm, gain_ref, emb_hbm, ids_hbm, q_hbm, dh_hbm, x_hbm, dz_hbm, fin_ref,
+    for u in range(tokens):
+        one_token(first + u)
+
+
+def kernel(n_tp, hid_hbm, gain_ref, emb_hbm, ids_hbm, q_hbm, dh_hbm, de_hbm, fin_ref,
            hid, emb, ids, q, xs, z, dz, lz_s, lo_s, code_s, qh_s, qm_s, ql_s, dense, part, sib_buf, ring_buf,
-           grad, dh_s, dw_acc, loss_acc, slz_acc, stat_buf, fin_buf,
-           in_sem, emb_sem, out_sem, dh_sem, x_sem, stat_send, stat_recv, fin_send, fin_recv, send_sem, recv_sem):
+           grad, dh_s, de_buf, dw_acc, loss_acc, slz_acc, stat_buf, fin_buf,
+           in_sem, emb_sem, de_sem, dh_sem, stat_send, stat_recv, fin_send, fin_recv, send_sem, recv_sem):
     tokens, width = hid.shape
     vocab = emb.shape[0]
     groups = vocab // LANES
@@ -94,15 +92,11 @@
         inv = lax.rsqrt(jnp.mean(h * h, axis=1, keepdims=True) + 1e-6)
         xs[rows, :] = (h * inv * gain).astype(jnp.bfloat16)
 
-    put_x = pltpu.make_async_copy(xs, x_hbm, x_sem)
-    put_x.start()
-
     @pl.loop(0, vocab // BLOCK)
     def _(b):
         get_emb(b).wait()
         rows = pl.ds(pl.multiple_of(b * BLOCK, BLOCK), BLOCK)
-        for r in range(0, tokens, min(512, tokens)):
-            z[b, pl.ds(r, min(512, tokens)), :] = lax.dot_general(xs[pl.ds(r, min(512, tokens)), :], emb[rows, :], (((1,), (1,)), ((), ())), preferred_element_type=jnp.float32)
+        z[b] = lax.dot_general(xs[...], emb[rows, :], (((1,), (1,)), ((), ())), preferred_element_type=jnp.float32)
 
     eye = lax.broadcasted_iota(jnp.int32, (LANES, LANES), 0) == lax.broadcasted_iota(jnp.int32, (LANES, LANES), 1)
 
@@ -154,8 +148,16 @@
             qm_s[rows, :] = wm
             ql_s[rows, :] = rest - wm
 
+    blocks = CHUNK // SUB
+
+    def targets(i):
+        build_targets(lo_s, code_s, (qh_s, qm_s, ql_s), dense, i * SUB, SUB, groups)
+
     prepare(0)
-    build_targets(lo_s, code_s, (qh_s, qm_s, ql_s), dense, 0, CHUNK, groups)
+
+    @pl.loop(0, blocks)
+    def _(i):
+        targets(i)
 
     for d in range(1, n_tp):
         everyone(stat_buf, stat_send, stat_recv, d).wait_recv()
@@ -198,36 +200,40 @@
         return pltpu.make_async_remote_copy(src_ref=src, dst_ref=dst, send_sem=send_sem.at[c, kind], recv_sem=recv_sem.at[c, kind],
                                             device_id=(dp, peer), device_id_type=MESH)
 
-    def put_dz(c):
-        rows = pl.ds(pl.multiple_of(c * CHUNK, CHUNK), CHUNK)
-        return pltpu.make_async_copy(dz.at[rows], dz_hbm.at[rows], out_sem.at[c])
+    def put_de(k):
+        rows = pl.ds(pl.multiple_of(k * BLOCK, BLOCK), BLOCK)
+        return pltpu.make_async_copy(de_buf.at[lax.rem(k, 2)], de_hbm.at[rows], de_sem.at[k])
 
     def put_dh(c):
         rows = pl.ds(pl.multiple_of(c * CHUNK, CHUNK), CHUNK)
         return pltpu.make_async_copy(dh_s.at[rows], dh_hbm.at[rows], dh_sem.at[c])
 
-    def compute(c):
-        sub = 32
-        first = pl.multiple_of(c * CHUNK, CHUNK)
-
-        @pl.loop(0, CHUNK // sub)
-        def _(i):
-            r = pl.multiple_of(i * sub, sub)
-            rows = pl.ds(pl.multiple_of(first + r, sub), sub)
-            lz = lz_s[rows, :]
-            s = jnp.broadcast_to(jnp.sum(q[rows, :], axis=1, keepdims=True) * scale, (sub, LANES))
-            acc = jnp.zeros((8, LANES), jnp.float32)
-            for g in range(groups):
-                v = z[g // 2, rows, pl.ds((g % 2) * LANES, LANES)]
-                target = dense[pl.ds(r * (groups + 1) + g, sub, stride=groups + 1), :]
-                dz[rows, pl.ds(g * LANES, LANES)] = (jnp.exp(v - lz) * s - target).astype(jnp.bfloat16)
-                acc += jnp.sum((target * v).reshape(sub // 8, 8, LANES), axis=0)
-            loss_acc[...] += acc
-            slz_acc[...] += jnp.sum((s * lz).reshape(sub // 8, 8, LANES), axis=0)
-
-        put_dz(c).start()
-        part[c] = jnp.dot(dz[pl.ds(first, CHUNK), :], emb[...], preferred_element_type=jnp.float32)
+    def make_dz(c, i):
+        r = pl.multiple_of(i * SUB, SUB)
+        rows = pl.ds(pl.multiple_of(c * CHUNK + r, SUB), SUB)
+        lz = lz_s[rows, :]
+        s = jnp.broadcast_to(jnp.sum(q[rows, :], axis=1, keepdims=True) * scale, (SUB, LANES))
+        acc = jnp.zeros((8, LANES), jnp.float32)
+        for g in range(groups):
+            v = z[g // 2, rows, pl.ds((g % 2) * LANES, LANES)]
+            target = dense[pl.ds(r * (groups + 1) + g, SUB, stride=groups + 1), :]
+            dz[rows, pl.ds(g * LANES, LANES)] = (jnp.exp(v - lz) * s - target).astype(jnp.bfloat16)
+            acc += jnp.sum((target * v).reshape(SUB // 8, 8, LANES), axis=0)
+        loss_acc[...] += acc
+        slz_acc[...] += jnp.sum((s * lz).reshape(SUB // 8, 8, LANES), axis=0)
+
+    def make_dx(c):
+        part[c] = jnp.dot(dz[pl.ds(pl.multiple_of(c * CHUNK, CHUNK), CHUNK), :], emb[...], preferred_element_type=jnp.float32)
         rdma(c, K_SIB).start()
+
+    def make_de(k):
+        @pl.when(k >= 2)
+        def _():
+            put_de(k - 2).wait()
+
+        cols = pl.ds(pl.multiple_of(k * BLOCK, BLOCK), BLOCK)
+        de_buf[lax.rem(k, 2)] = lax.dot_general(dz[:, cols], xs[...], (((0,), (0,)), ((), ())), preferred_element_type=jnp.float32)
+        put_de(k).start()
 
     def part_rows(first, count):
         return pl.ds(pl.multiple_of(first, 8), count)
@@ -289,7 +295,14 @@
         dh_s[pl.ds(pl.multiple_of(c * CHUNK, CHUNK), CHUNK), :] = grad[c].astype(jnp.bfloat16)
         put_dh(c).start()
 
-    stages = ((LAG_F, stage_f), (LAG_E, stage_e), (LAG_D, stage_d), (LAG_C, stage_c), (LAG_B, stage_b), (LAG_A, stage_a), (0, compute))
+    stages = ((LAG_F, stage_f), (LAG_E, stage_e), (LAG_D, stage_d), (LAG_C, stage_c), (LAG_B, stage_b), (LAG_A, stage_a))
+
+    @pl.loop(0, blocks - 1)
+    def _(i):
+        make_dz(0, i)
+
+    de_blocks = vocab // BLOCK
+    last = SLOTS * (chunks - 1)
 
     @pl.loop(0, SLOTS * chunks + LAG_F - SLOTS + 1)
     def _(slot):
@@ -303,13 +316,35 @@
         phase = lax.rem(slot, SLOTS)
         c = slot // SLOTS
 
-        @pl.when((phase == 1) & (c < chunks - 1))
+        @pl.when((phase == 0) & (c < chunks - 1))
         def _():
             prepare(c + 1)
 
-        @pl.when((phase >= 1) & (c < chunks - 1))
-        def _():
-            build_targets(lo_s, code_s, (qh_s, qm_s, ql_s), dense, (phase - 1) * (CHUNK // 2), CHUNK // 2, groups)
+        @pl.when((c < chunks - 1))
+        def _():
+            first = jnp.where(phase == 0, 0, jnp.where(phase == 1, 1, (blocks + 1) // 2))
+            count = jnp.where(phase == 0, 1, jnp.where(phase == 1, (blocks + 1) // 2 - 1, blocks - (blocks + 1) // 2))
+
+            @pl.loop(0, count)
+            def _(i):
+                block = (c + 1) * blocks + first + i - 1
+                make_dz(block // blocks, lax.rem(block, blocks))
+                targets(first + i)
+
+        @pl.when(slot == last)
+        def _():
+            make_dz(chunks - 1, blocks - 1)
+
+        @pl.when((phase == 0) & (c < chunks))
+        def _():
+            make_dx(c)
+
+        k = slot - last - 1
+        block = k - (k + 2) // 4
+
+        @pl.when((k >= 0) & (lax.rem(k + 3, 4) != 0) & (block < de_blocks))
+        def _():
+            make_de(block)
 
     for d in range(1, n_tp):
         everyone(fin_buf, fin_send, fin_recv, d).wait_recv()
@@ -327,10 +362,10 @@
     def _(c):
         for kind in range(KINDS):
             rdma(c, kind).wait_send()
-        put_dz(c).wait()
         put_dh(c).wait()
 
-    put_x.wait()
+    for k in (de_blocks - 2, de_blocks - 1):
+        put_de(k).wait()
 
 
 def solution(mesh):
@@ -346,26 +381,24 @@
         f32, bf16 = jnp.float32, jnp.bfloat16
         dma = pltpu.SemaphoreType.DMA
         hbm, vmem = pl.BlockSpec(memory_space=pl.ANY), pl.BlockSpec(memory_space=pltpu.VMEM)
-        dh, x_in, grad_z, fin = pl.pallas_call(
+        dh, grad_block, fin = pl.pallas_call(
             functools.partial(kernel, n_tp),
-            out_shape=(jax.ShapeDtypeStruct((tokens, width), bf16), jax.ShapeDtypeStruct((tokens, width), bf16),
-                       jax.ShapeDtypeStruct((tokens, vocab), bf16), jax.ShapeDtypeStruct((16, LANES), f32)),
+            out_shape=(jax.ShapeDtypeStruct((tokens, width), bf16), jax.ShapeDtypeStruct((vocab, width), f32), jax.ShapeDtypeStruct((16, LANES), f32)),
             in_specs=[hbm, vmem, hbm, hbm, hbm],
-            out_specs=(hbm, hbm, hbm, vmem),
+            out_specs=(hbm, hbm, vmem),
             scratch_shapes=[
                 pltpu.VMEM((tokens, width), bf16), pltpu.VMEM((vocab, width), bf16), pltpu.VMEM((tokens, count), jnp.int32), pltpu.VMEM((tokens, count), f32),
                 pltpu.VMEM((tokens, width), bf16), pltpu.VMEM((vocab // BLOCK, tokens, BLOCK), f32), pltpu.VMEM((tokens, vocab), bf16), pltpu.VMEM((tokens, LANES), f32),
                 *[pltpu.VMEM((CHUNK, count), f32)] * 5, pltpu.VMEM((CHUNK * (vocab // LANES + 1), LANES), f32),
                 pltpu.VMEM((chunks, CHUNK, width), f32), pltpu.VMEM((chunks, half, width), f32), pltpu.VMEM((chunks, 6, bit, width), f32),
-                pltpu.VMEM((chunks, CHUNK, width), f32), pltpu.VMEM((tokens, width), bf16),
+                pltpu.VMEM((chunks, CHUNK, width), f32), pltpu.VMEM((tokens, width), bf16), pltpu.VMEM((2, BLOCK, width), f32),
                 pltpu.VMEM((8, width), f32), pltpu.VMEM((8, LANES), f32), pltpu.VMEM((8, LANES), f32),
                 pltpu.VMEM((n_tp, 2 * tokens // LANES, LANES), f32), pltpu.VMEM((n_tp, 16, LANES), f32),
-                dma((3,)), dma((vocab // BLOCK,)), dma((chunks,)), dma((chunks,)), dma(()),
+                dma((3,)), dma((vocab // BLOCK,)), dma((vocab // BLOCK,)), dma((chunks,)),
                 dma((n_tp - 1,)), dma((n_tp - 1,)), dma((n_tp - 1,)), dma((n_tp - 1,)), dma((chunks, KINDS)), dma((chunks, KINDS)),
             ],
             compiler_params=pltpu.CompilerParams(collective_id=0, has_side_effects=True, vmem_limit_bytes=60 * 2**20),
         )(hidden, norm_gain, emb_block, teacher_ids, teacher_q)
-        grad_block = lax.dot_general(grad_z, x_in, (((0,), (0,)), ((), ())), preferred_element_type=f32)
         lanes = width // LANES
         return fin[lanes, :1], dh, fin[:lanes].reshape(-1), grad_block
 

time: 97.4 us -> 98.5 us (1.011)
  local copies, waits for them, and re-layouts: 2.53 us -> 13.8 us
  matrix products: 10.5 us -> 0 us
    dot_general x1 -> x0, matrix products: 10.5 us -> none  [local_step(): lax.dot_general(grad_z, x_in, (((0,), (0,)), ((), ())), preferred_element...]
    unnamed x5 -> x2, local copies, waits for them, and re-layouts: 1.41 us -> 11.3 us
where the time goes in v4:
time: 98.5 us; the launch traced here: 98.2 us
  Pallas kernels  83.8 us (85%)
  local copies, waits for them, and re-layouts  13.8 us (14%)
    pallas_call x1, Pallas kernels, local_step(): pl.pallas_call(functools.partial(kernel, n_tp), out_shape=(jax.ShapeDtype...  83.8 us
    unnamed x2, local copies, waits for them, and re-layouts  11.3 us

profile of v4, /device:TPU:81, one launch (start us, length us, event | category | flops | bytes accessed | tf_op | source)
XLA Modules:
  0.0 98.2 jit_solution(4040949994588225537)
XLA Ops:
  0.6 83.8 %shard_map.84 = (bf16[1024,1152]{1,0:T(8,128)(2,1)}, f32[2048,1152]{1,0:T(8,128)}, f32[16,128]{1,0:T(8,128)}) custom-call(bf16[1024,1152]{1,0:T(8,128)(2,1)} %hid_hbm.1, f32[1152]{0:T(1024)} %gain_ref.1, bf16[2048,1152]{1,0:T(8,128)(2,1)} %emb_hbm.1, s32[1024,256]{1,0:T(8,128)} %ids_hbm.1, f32[1024,256]{1,0:T(8,128)} %q_hbm.1), custom_call_target="tpu_custom_call" | custom-call | tf_op jit(solution)/shard_map/pallas_call | solution.py:384
  84.5 1.2 %slice.6 = f32[1,1]{1,0:T(1,128)} slice(f32[16,128]{1,0:T(8,128)} %get-tuple-element.7), slice={[9:10], [0:1]} | slice | bytes 8 | tf_op jit(solution)/shard_map/slice | solution.py:403
  85.7 1.3 %slice_bitcast_fusion = f32[1152]{0:T(1024)} fusion(f32[16,128]{1,0:T(8,128)} %get-tuple-element.7), kind=kLoop, calls=%fused_computation | loop fusion | bytes 9216 | tf_op jit(solution)/shard_map/reshape | solution.py:403
  87.0 3.2 %copy.11 = bf16[1024,1152]{1,0:T(8,128)(2,1)} copy(bf16[1024,1152]{1,0:T(8,128)(2,1)} %get-tuple-element.15) | data formatting | bytes 4718592
  90.2 8.0 %copy.12 = f32[2048,1152]{1,0:T(8,128)} copy(f32[2048,1152]{1,0:T(8,128)} %get-tuple-element.17) | data formatting | bytes 18874368

commit v5 on v4

--- a/solution.py
+++ b/solution.py
@@ -19,10 +19,11 @@
 KINDS = 15
 
 
-def build_targets(lo_ref, code_ref, pieces, dense_ref, first, tokens, groups):
+def build_targets(lo_ref, code_ref, dense_ref, first, tokens, groups):
     count = lo_ref.shape[1]
     sub, half = 16, LANES // 2
     base = lax.broadcasted_iota(jnp.int32, (sub, count), 0).astype(jnp.float32).astype(jnp.bfloat16)
+    slot = (lax.broadcasted_iota(jnp.int32, (sub, count), 1) + 1).astype(jnp.float32).astype(jnp.bfloat16)
     zero = jnp.zeros((sub, count), jnp.bfloat16)
     one = jnp.ones((sub, count), jnp.bfloat16)
 
@@ -31,22 +32,24 @@
 
     def one_token(n):
         lo, code = row(lo_ref, n), row(code_ref, n)
-        weights = [row(ref, n) for ref in pieces]
         low_hot = jnp.concatenate([jnp.where(lo == base + jnp.bfloat16(sub * k), one, zero) for k in range(half // sub)], axis=0)
-        here = [code == base + jnp.bfloat16(sub * k) for k in range(2 * groups // sub)]
-        lhs = jnp.concatenate([jnp.where(h, w, zero) for w in weights for h in here], axis=0)
+        lhs = jnp.concatenate([jnp.where(code == base + jnp.bfloat16(sub * k), slot, zero) for k in range(2 * groups // sub)], axis=0)
         out = lax.dot_general(lhs, low_hot, (((1,), (1,)), ((), ())), preferred_element_type=jnp.float32)
-        out = out[:2 * groups] + out[2 * groups:4 * groups] + out[4 * groups:]
         dense_ref[pl.ds(n * (groups + 1), groups), :] = jnp.concatenate([out[:groups], out[groups:]], axis=1)
 
     for u in range(tokens):
         one_token(first + u)
 
 
-def kernel(n_tp, hid_hbm, gain_ref, emb_hbm, ids_hbm, q_hbm, dh_hbm, de_hbm, fin_ref,
-           hid, emb, ids, q, xs, z, dz, lz_s, lo_s, code_s, qh_s, qm_s, ql_s, dense, part, sib_buf, ring_buf,
-           grad, dh_s, de_buf, dw_acc, loss_acc, slz_acc, stat_buf, fin_buf,
-           in_sem, emb_sem, de_sem, dh_sem, stat_send, stat_recv, fin_send, fin_recv, send_sem, recv_sem):
+def take(table, lane):
+    dims = lax.GatherDimensionNumbers(offset_dims=(), collapsed_slice_dims=(1,), start_index_map=(1,), operand_batching_dims=(0,), start_indices_batching_dims=(0,))
+    return lax.gather(table, lane[..., None], dims, slice_sizes=(1, 1), mode=lax.GatherScatterMode.PROMISE_IN_BOUNDS)
+
+
+def kernel(n_tp, hid_hbm, gain_ref, emb_hbm, ids_hbm, q_hbm, dh_hbm, x_hbm, dz_hbm, fin_ref,
+           hid, emb, ids, q, xs, z, dz, lz_s, lo_s, code_s, dense, part, sib_buf, ring_buf,
+           grad, dh_s, dw_acc, loss_acc, slz_acc, stat_buf, fin_buf,
+           in_sem, emb_sem, out_sem, dh_sem, x_sem, stat_send, stat_recv, fin_send, fin_recv, send_sem, recv_sem):
     tokens, width = hid.shape
     vocab = emb.shape[0]
     groups = vocab // LANES
@@ -96,7 +99,9 @@
     def _(b):
         get_emb(b).wait()
         rows = pl.ds(pl.multiple_of(b * BLOCK, BLOCK), BLOCK)
-        z[b] = lax.dot_general(xs[...], emb[rows, :], (((1,), (1,)), ((), ())), preferred_element_type=jnp.float32)
+        m = min(512, tokens)
+        for r in range(0, tokens, m):
+            z[b, pl.ds(r, m), :] = lax.dot_general(xs[pl.ds(r, m), :], emb[rows, :], (((1,), (1,)), ((), ())), preferred_element_type=jnp.float32)
 
     eye = lax.broadcasted_iota(jnp.int32, (LANES, LANES), 0) == lax.broadcasted_iota(jnp.int32, (LANES, LANES), 1)
 
@@ -140,18 +145,11 @@
             lo_s[rows, :] = jnp.bitwise_and(lid, LANES // 2 - 1).astype(jnp.float32)
             code = jnp.right_shift(lid, 7) + groups * jnp.bitwise_and(jnp.right_shift(lid, 6), 1)
             code_s[rows, :] = jnp.where((lid >= 0) & (lid < vocab), code, -1).astype(jnp.float32)
-            w = q[src, :] * scale
-            wh = w.astype(jnp.bfloat16).astype(jnp.float32)
-            rest = w - wh
-            wm = rest.astype(jnp.bfloat16).astype(jnp.float32)
-            qh_s[rows, :] = wh
-            qm_s[rows, :] = wm
-            ql_s[rows, :] = rest - wm
 
     blocks = CHUNK // SUB
 
     def targets(i):
-        build_targets(lo_s, code_s, (qh_s, qm_s, ql_s), dense, i * SUB, SUB, groups)
+        build_targets(lo_s, code_s, dense, i * SUB, SUB, groups)
 
     prepare(0)
 
@@ -200,9 +198,12 @@
         return pltpu.make_async_remote_copy(src_ref=src, dst_ref=dst, send_sem=send_sem.at[c, kind], recv_sem=recv_sem.at[c, kind],
                                             device_id=(dp, peer), device_id_type=MESH)
 
-    def put_de(k):
-        rows = pl.ds(pl.multiple_of(k * BLOCK, BLOCK), BLOCK)
-        return pltpu.make_async_copy(de_buf.at[lax.rem(k, 2)], de_hbm.at[rows], de_sem.at[k])
+    put_x = pltpu.make_async_copy(xs, x_hbm, x_sem)
+    put_x.start()
+
+    def put_dz(c):
+        rows = pl.ds(pl.multiple_of(c * CHUNK, CHUNK), CHUNK)
+        return pltpu.make_async_copy(dz.at[rows], dz_hbm.at[rows], out_sem.at[c])
 
     def put_dh(c):
         rows = pl.ds(pl.multiple_of(c * CHUNK, CHUNK), CHUNK)
@@ -212,11 +213,15 @@
         r = pl.multiple_of(i * SUB, SUB)
         rows = pl.ds(pl.multiple_of(c * CHUNK + r, SUB), SUB)
         lz = lz_s[rows, :]
-        s = jnp.broadcast_to(jnp.sum(q[rows, :], axis=1, keepdims=True) * scale, (SUB, LANES))
+        q_lo, q_hi = q[rows, :LANES] * scale, q[rows, LANES:] * scale
+        s = jnp.broadcast_to(jnp.sum(q_lo + q_hi, axis=1, keepdims=True), (SUB, LANES))
         acc = jnp.zeros((8, LANES), jnp.float32)
         for g in range(groups):
             v = z[g // 2, rows, pl.ds((g % 2) * LANES, LANES)]
-            target = dense[pl.ds(r * (groups + 1) + g, SUB, stride=groups + 1), :]
+            slot = dense[pl.ds(r * (groups + 1) + g, SUB, stride=groups + 1), :]
+            lane = slot.astype(jnp.int32) - 1
+            low = jnp.bitwise_and(lane, LANES - 1)
+            target = jnp.where(slot < 0.5, 0.0, jnp.where(lane < LANES, take(q_lo, low), take(q_hi, low)))
             dz[rows, pl.ds(g * LANES, LANES)] = (jnp.exp(v - lz) * s - target).astype(jnp.bfloat16)
             acc += jnp.sum((target * v).reshape(SUB // 8, 8, LANES), axis=0)
         loss_acc[...] += acc
@@ -225,15 +230,7 @@
     def make_dx(c):
         part[c] = jnp.dot(dz[pl.ds(pl.multiple_of(c * CHUNK, CHUNK), CHUNK), :], emb[...], preferred_element_type=jnp.float32)
         rdma(c, K_SIB).start()
-
-    def make_de(k):
-        @pl.when(k >= 2)
-        def _():
-            put_de(k - 2).wait()
-
-        cols = pl.ds(pl.multiple_of(k * BLOCK, BLOCK), BLOCK)
-        de_buf[lax.rem(k, 2)] = lax.dot_general(dz[:, cols], xs[...], (((0,), (0,)), ((), ())), preferred_element_type=jnp.float32)
-        put_de(k).start()
+        put_dz(c).start()
 
     def part_rows(first, count):
         return pl.ds(pl.multiple_of(first, 8), count)
@@ -301,7 +298,6 @@
     def _(i):
         make_dz(0, i)
 
-    de_blocks = vocab // BLOCK
     last = SLOTS * (chunks - 1)
 
     @pl.loop(0, SLOTS * chunks + LAG_F - SLOTS + 1)
@@ -338,13 +334,6 @@
         @pl.when((phase == 0) & (c < chunks))
         def _():
             make_dx(c)
-
-        k = slot - last - 1
-        block = k - (k + 2) // 4
-
-        @pl.when((k >= 0) & (lax.rem(k + 3, 4) != 0) & (block < de_blocks))
-        def _():
-            make_de(block)
 
     for d in range(1, n_tp):
         everyone(fin_buf, fin_send, fin_recv, d).wait_recv()
@@ -363,9 +352,9 @@
         for kind in range(KINDS):
             rdma(c, kind).wait_send()
         put_dh(c).wait()
-
-    for k in (de_blocks - 2, de_blocks - 1):
-        put_de(k).wait()
+        put_dz(c).wait()
+
+    put_x.wait()
 
 
 def solution(mesh):
@@ -381,24 +370,26 @@
         f32, bf16 = jnp.float32, jnp.bfloat16
         dma = pltpu.SemaphoreType.DMA
         hbm, vmem = pl.BlockSpec(memory_space=pl.ANY), pl.BlockSpec(memory_space=pltpu.VMEM)
-        dh, grad_block, fin = pl.pallas_call(
+        dh, x_in, grad_z, fin = pl.pallas_call(
             functools.partial(kernel, n_tp),
-            out_shape=(jax.ShapeDtypeStruct((tokens, width), bf16), jax.ShapeDtypeStruct((vocab, width), f32), jax.ShapeDtypeStruct((16, LANES), f32)),
+            out_shape=(jax.ShapeDtypeStruct((tokens, width), bf16), jax.ShapeDtypeStruct((tokens, width), bf16),
+                       jax.ShapeDtypeStruct((tokens, vocab), bf16), jax.ShapeDtypeStruct((16, LANES), f32)),
             in_specs=[hbm, vmem, hbm, hbm, hbm],
-            out_specs=(hbm, hbm, vmem),
+            out_specs=(hbm, hbm, hbm, vmem),
             scratch_shapes=[
                 pltpu.VMEM((tokens, width), bf16), pltpu.VMEM((vocab, width), bf16), pltpu.VMEM((tokens, count), jnp.int32), pltpu.VMEM((tokens, count), f32),
                 pltpu.VMEM((tokens, width), bf16), pltpu.VMEM((vocab // BLOCK, tokens, BLOCK), f32), pltpu.VMEM((tokens, vocab), bf16), pltpu.VMEM((tokens, LANES), f32),
-                *[pltpu.VMEM((CHUNK, count), f32)] * 5, pltpu.VMEM((CHUNK * (vocab // LANES + 1), LANES), f32),
+                *[pltpu.VMEM((CHUNK, count), f32)] * 2, pltpu.VMEM((CHUNK * (vocab // LANES + 1), LANES), f32),
                 pltpu.VMEM((chunks, CHUNK, width), f32), pltpu.VMEM((chunks, half, width), f32), pltpu.VMEM((chunks, 6, bit, width), f32),
-                pltpu.VMEM((chunks, CHUNK, width), f32), pltpu.VMEM((tokens, width), bf16), pltpu.VMEM((2, BLOCK, width), f32),
+                pltpu.VMEM((chunks, CHUNK, width), f32), pltpu.VMEM((tokens, width), bf16),
                 pltpu.VMEM((8, width), f32), pltpu.VMEM((8, LANES), f32), pltpu.VMEM((8, LANES), f32),
                 pltpu.VMEM((n_tp, 2 * tokens // LANES, LANES), f32), pltpu.VMEM((n_tp, 16, LANES), f32),
-                dma((3,)), dma((vocab // BLOCK,)), dma((vocab // BLOCK,)), dma((chunks,)),
+                dma((3,)), dma((vocab // BLOCK,)), dma((chunks,)), dma((chunks,)), dma(()),
                 dma((n_tp - 1,)), dma((n_tp - 1,)), dma((n_tp - 1,)), dma((n_tp - 1,)), dma((chunks, KINDS)), dma((chunks, KINDS)),
             ],
             compiler_params=pltpu.CompilerParams(collective_id=0, has_side_effects=True, vmem_limit_bytes=60 * 2**20),
         )(hidden, norm_gain, emb_block, teacher_ids, teacher_q)
+        grad_block = lax.dot_general(grad_z, x_in, (((0,), (0,)), ((), ())), preferred_element_type=f32)
         lanes = width // LANES
         return fin[lanes, :1], dh, fin[:lanes].reshape(-1), grad_block
 

time: 98.5 us -> 97.2 us (0.987)
  local copies, waits for them, and re-layouts: 13.8 us -> 2.53 us
  matrix products: 0 us -> 10.5 us
    dot_general x0 -> x1, matrix products: none -> 10.5 us  [local_step(): lax.dot_general(grad_z, x_in, (((0,), (0,)), ((), ())), preferred_element...]
    unnamed x2 -> x5, local copies, waits for them, and re-layouts: 11.3 us -> 1.41 us
where the time goes in v5:
time: 97.2 us; the launch traced here: 97.1 us
  Pallas kernels  83.4 us (86%)
  matrix products  10.5 us (11%)
  local copies, waits for them, and re-layouts  2.53 us (3%)
    pallas_call x1, Pallas kernels, local_step(): pl.pallas_call(functools.partial(kernel, n_tp), out_shape=(jax.ShapeDtype...  83.4 us
    dot_general x1, matrix products, local_step(): lax.dot_general(grad_z, x_in, (((0,), (0,)), ((), ())), preferred_element...  10.5 us

profile of v5, /device:TPU:81, one launch (start us, length us, event | category | flops | bytes accessed | tf_op | source)
XLA Modules:
  0.0 97.1 jit_solution(6643318100994716744)
XLA Ops:
  0.6 83.4 %shard_map.84 = (bf16[1024,1152]{1,0:T(8,128)(2,1)}, bf16[1024,1152]{1,0:T(8,128)(2,1)}, bf16[1024,2048]{1,0:T(8,128)(2,1)}, f32[16,128]{1,0:T(8,128)}) custom-call(bf16[1024,1152]{1,0:T(8,128)(2,1)} %hid_hbm.1, f32[1152]{0:T(1024)} %gain_ref.1, bf16[2048,1152]{1,0:T(8,128)(2,1)} %emb_hbm.1, s32[1024,256]{1,0:T(8,128)} %ids_hbm.1, f32[1024,256]{1,0:T(8,128)} %q_hbm.1), custom_call_target="tpu_custom_call" | custom-call | tf_op jit(solution)/shard_map/pallas_call | solution.py:373
  84.0 0.0 copy-start.1
  84.0 0.0 copy-start
  84.0 10.5 %fusion = f32[2048,1152]{1,0:T(8,128)} fusion(bf16[1024,2048]{1,0:T(8,128)(2,1)} %get-tuple-element.10, bf16[1024,1152]{1,0:T(8,128)(2,1)} %get-tuple-element.11), kind=kOutput, calls=%fused_computation.1 | convolution fusion | flops 4831838208 | bytes 15990784 | tf_op jit(solution)/shard_map/dot_general | solution.py:392
  94.6 0.0 copy-done.1
  94.6 0.6 slice_bitcast_fusion
  95.2 0.5 slice.6
  95.7 0.0 copy-done
  95.7 1.4 %copy.10 = bf16[1024,1152]{1,0:T(8,128)(2,1)} copy(bf16[1024,1152]{1,0:T(8,128)(2,1)S(1)} %copy-done) | data formatting | bytes 4718592
Async XLA Ops:
  84.0 10.5 %copy-start.1 = (f32[16,128]{1,0:T(8,128)S(1)}, f32[16,128]{1,0:T(8,128)}, u32[]{:S(2)}) copy-start(f32[16,128]{1,0:T(8,128)} %get-tuple-element.8) | copy-start | bytes 24580
  84.0 11.7 %copy-start = (bf16[1024,1152]{1,0:T(8,128)(2,1)S(1)}, bf16[1024,1152]{1,0:T(8,128)(2,1)}, u32[]{:S(2)}) copy-start(bf16[1024,1152]{1,0:T(8,128)(2,1)} %get-tuple-element.17) | copy-start | bytes 7077892

commit v6 on v5

--- a/solution.py
+++ b/solution.py
@@ -47,7 +47,7 @@
 
 
 def kernel(n_tp, hid_hbm, gain_ref, emb_hbm, ids_hbm, q_hbm, dh_hbm, x_hbm, dz_hbm, fin_ref,
-           hid, emb, ids, q, xs, z, dz, lz_s, lo_s, code_s, dense, part, sib_buf, ring_buf,
+           hid, emb, ids, q, xs, z, dz, lz_s, peak_s, sum_s, lo_s, code_s, dense, part, sib_buf, ring_buf,
            grad, dh_s, dw_acc, loss_acc, slz_acc, stat_buf, fin_buf,
            in_sem, emb_sem, out_sem, dh_sem, x_sem, stat_send, stat_recv, fin_send, fin_recv, send_sem, recv_sem):
     tokens, width = hid.shape
@@ -80,12 +80,12 @@
         return pltpu.make_async_copy(emb_hbm.at[rows], emb.at[rows], emb_sem.at[b])
 
     get_hid.start()
+    get_hid.wait()
     for b in range(vocab // BLOCK):
         get_emb(b).start()
     get_ids.start()
     get_q.start()
 
-    get_hid.wait()
     gain = 1.0 + gain_ref[...].reshape(1, width)
 
     @pl.loop(0, tokens // 32)
@@ -95,13 +95,34 @@
         inv = lax.rsqrt(jnp.mean(h * h, axis=1, keepdims=True) + 1e-6)
         xs[rows, :] = (h * inv * gain).astype(jnp.bfloat16)
 
-    @pl.loop(0, vocab // BLOCK)
+    peak_s[...] = jnp.full(peak_s.shape, -jnp.inf, jnp.float32)
+    sum_s[...] = jnp.zeros(sum_s.shape, jnp.float32)
+
+    def lane_stats(b, first, count):
+        for r in range(0, count, 32):
+            rows = pl.ds(first + r, 32)
+            tiles = [z[b, rows, pl.ds(g * LANES, LANES)] for g in range(BLOCK // LANES)]
+            old = peak_s[rows, :]
+            new = functools.reduce(jnp.maximum, tiles, old)
+            sum_s[rows, :] = functools.reduce(jnp.add, [jnp.exp(v - new) for v in tiles], sum_s[rows, :] * jnp.exp(old - new))
+            peak_s[rows, :] = new
+
+    m = min(512, tokens)
+
+    def logits(b, r):
+        rows = pl.ds(pl.multiple_of(b * BLOCK, BLOCK), BLOCK)
+        z[b, pl.ds(r, m), :] = lax.dot_general(xs[pl.ds(r, m), :], emb[rows, :], (((1,), (1,)), ((), ())), preferred_element_type=jnp.float32)
+
+    get_emb(0).wait()
+    for r in range(0, tokens, m):
+        logits(0, r)
+
+    @pl.loop(1, vocab // BLOCK)
     def _(b):
         get_emb(b).wait()
-        rows = pl.ds(pl.multiple_of(b * BLOCK, BLOCK), BLOCK)
-        m = min(512, tokens)
         for r in range(0, tokens, m):
-            z[b, pl.ds(r, m), :] = lax.dot_general(xs[pl.ds(r, m), :], emb[rows, :], (((1,), (1,)), ((), ())), preferred_element_type=jnp.float32)
+            lane_stats(b - 1, r, m)
+            logits(b, r)
 
     eye = lax.broadcasted_iota(jnp.int32, (LANES, LANES), 0) == lax.broadcasted_iota(jnp.int32, (LANES, LANES), 1)
 
@@ -112,16 +133,14 @@
 
     @pl.loop(0, stat_rows)
     def _(t):
-        for u in range(0, LANES, 32):
-            rows = pl.ds(pl.multiple_of(t * LANES + u, 32), 32)
-            tiles = [z[g // 2, rows, pl.ds((g % 2) * LANES, LANES)] for g in range(groups)]
-            peak = functools.reduce(jnp.maximum, tiles)
-            peak = jnp.broadcast_to(jnp.max(peak, axis=1, keepdims=True), (32, LANES))
-            total = functools.reduce(jnp.add, [jnp.exp(v - peak) for v in tiles])
-            lz_s[rows, :] = peak
-            dense[pl.ds(u, 32), :] = jnp.broadcast_to(jnp.sum(total, axis=1, keepdims=True), (32, LANES))
-        stat_buf[me, pl.ds(t, 1), :] = as_row(lz_s[pl.ds(pl.multiple_of(t * LANES, LANES), LANES), :])
-        stat_buf[me, pl.ds(stat_rows + t, 1), :] = as_row(dense[pl.ds(0, LANES), :])
+        first = pl.multiple_of(t * LANES, LANES)
+        lane_stats(vocab // BLOCK - 1, first, LANES)
+        rows = pl.ds(first, LANES)
+        lane_peak = peak_s[rows, :]
+        peak = jnp.broadcast_to(jnp.max(lane_peak, axis=1, keepdims=True), (LANES, LANES))
+        total = jnp.sum(sum_s[rows, :] * jnp.exp(lane_peak - peak), axis=1, keepdims=True)
+        stat_buf[me, pl.ds(t, 1), :] = as_row(peak)
+        stat_buf[me, pl.ds(stat_rows + t, 1), :] = as_row(jnp.broadcast_to(total, (LANES, LANES)))
 
     def everyone(buf, send, recv, d):
         return pltpu.make_async_remote_copy(
@@ -378,7 +397,7 @@
             out_specs=(hbm, hbm, hbm, vmem),
             scratch_shapes=[
                 pltpu.VMEM((tokens, width), bf16), pltpu.VMEM((vocab, width), bf16), pltpu.VMEM((tokens, count), jnp.int32), pltpu.VMEM((tokens, count), f32),
-                pltpu.VMEM((tokens, width), bf16), pltpu.VMEM((vocab // BLOCK, tokens, BLOCK), f32), pltpu.VMEM((tokens, vocab), bf16), pltpu.VMEM((tokens, LANES), f32),
+                pltpu.VMEM((tokens, width), bf16), pltpu.VMEM((vocab // BLOCK, tokens, BLOCK), f32), pltpu.VMEM((tokens, vocab), bf16), *[pltpu.VMEM((tokens, LANES), f32)] * 3,
                 *[pltpu.VMEM((CHUNK, count), f32)] * 2, pltpu.VMEM((CHUNK * (vocab // LANES + 1), LANES), f32),
                 pltpu.VMEM((chunks, CHUNK, width), f32), pltpu.VMEM((chunks, half, width), f32), pltpu.VMEM((chunks, 6, bit, width), f32),
                 pltpu.VMEM((chunks, CHUNK, width), f32), pltpu.VMEM((tokens, width), bf16),

time: 97.2 us -> 95.7 us (0.985)
  Pallas kernels: 83.4 us -> 81.9 us
    pallas_call x1, Pallas kernels: 83.4 us -> 81.9 us  [local_step(): pl.pallas_call(functools.partial(kernel, n_tp), out_shape=(jax.ShapeDtype...]
where the time goes in v6:
time: 95.7 us; the launch traced here: 95.6 us
  Pallas kernels  81.9 us (86%)
  matrix products  10.5 us (11%)
  local copies, waits for them, and re-layouts  2.53 us (3%)
    pallas_call x1, Pallas kernels, local_step(): pl.pallas_call(functools.partial(kernel, n_tp), out_shape=(jax.ShapeDtype...  81.9 us
    dot_general x1, matrix products, local_step(): lax.dot_general(grad_z, x_in, (((0,), (0,)), ((), ())), preferred_element...  10.5 us

profile of v6, /device:TPU:81, one launch (start us, length us, event | category | flops | bytes accessed | tf_op | source)
XLA Modules:
  0.0 95.6 jit_solution(9084048251568633137)
XLA Ops:
  0.6 81.9 %shard_map.84 = (bf16[1024,1152]{1,0:T(8,128)(2,1)}, bf16[1024,1152]{1,0:T(8,128)(2,1)}, bf16[1024,2048]{1,0:T(8,128)(2,1)}, f32[16,128]{1,0:T(8,128)}) custom-call(bf16[1024,1152]{1,0:T(8,128)(2,1)} %hid_hbm.1, f32[1152]{0:T(1024)} %gain_ref.1, bf16[2048,1152]{1,0:T(8,128)(2,1)} %emb_hbm.1, s32[1024,256]{1,0:T(8,128)} %ids_hbm.1, f32[1024,256]{1,0:T(8,128)} %q_hbm.1), custom_call_target="tpu_custom_call" | custom-call | tf_op jit(solution)/shard_map/pallas_call | solution.py:392
  82.5 0.0 copy-start.1
  82.5 0.0 copy-start
  82.5 10.5 %fusion = f32[2048,1152]{1,0:T(8,128)} fusion(bf16[1024,2048]{1,0:T(8,128)(2,1)} %get-tuple-element.10, bf16[1024,1152]{1,0:T(8,128)(2,1)} %get-tuple-element.11), kind=kOutput, calls=%fused_computation.1 | convolution fusion | flops 4831838208 | bytes 15990784 | tf_op jit(solution)/shard_map/dot_general | solution.py:411
  93.1 0.0 copy-done.1
  93.1 0.6 slice_bitcast_fusion
  93.7 0.5 slice.6
  94.2 0.0 copy-done
  94.2 1.4 %copy.10 = bf16[1024,1152]{1,0:T(8,128)(2,1)} copy(bf16[1024,1152]{1,0:T(8,128)(2,1)S(1)} %copy-done) | data formatting | bytes 4718592
Async XLA Ops:
  82.5 10.5 %copy-start.1 = (f32[16,128]{1,0:T(8,128)S(1)}, f32[16,128]{1,0:T(8,128)}, u32[]{:S(2)}) copy-start(f32[16,128]{1,0:T(8,128)} %get-tuple-element.8) | copy-start | bytes 24580
  82.5 11.7 %copy-start = (bf16[1024,1152]{1,0:T(8,128)(2,1)S(1)}, bf16[1024,1152]{1,0:T(8,128)(2,1)}, u32[]{:S(2)}) copy-start(bf16[1024,1152]{1,0:T(8,128)(2,1)} %get-tuple-element.17) | copy-start | bytes 7077892

commit v7 on v6

--- a/solution.py
+++ b/solution.py
@@ -71,16 +71,21 @@
     for d in range(1, n_tp):
         pl.semaphore_signal(barrier, inc=1, device_id=(dp, lax.rem(me + d, n_tp)), device_id_type=MESH)
 
-    get_hid = pltpu.make_async_copy(hid_hbm, hid, in_sem.at[0])
-    get_ids = pltpu.make_async_copy(ids_hbm, ids, in_sem.at[1])
-    get_q = pltpu.make_async_copy(q_hbm, q, in_sem.at[2])
+    quarter = tokens // 4
+
+    def get_hid(i):
+        rows = pl.ds(pl.multiple_of(i * quarter, quarter), quarter)
+        return pltpu.make_async_copy(hid_hbm.at[rows], hid.at[rows], in_sem.at[2 + i])
+
+    get_ids = pltpu.make_async_copy(ids_hbm, ids, in_sem.at[0])
+    get_q = pltpu.make_async_copy(q_hbm, q, in_sem.at[1])
 
     def get_emb(b):
         rows = pl.ds(pl.multiple_of(b * BLOCK, BLOCK), BLOCK)
         return pltpu.make_async_copy(emb_hbm.at[rows], emb.at[rows], emb_sem.at[b])
 
-    get_hid.start()
-    get_hid.wait()
+    for i in range(4):
+        get_hid(i).start()
     for b in range(vocab // BLOCK):
         get_emb(b).start()
     get_ids.start()
@@ -88,12 +93,16 @@
 
     gain = 1.0 + gain_ref[...].reshape(1, width)
 
-    @pl.loop(0, tokens // 32)
+    @pl.loop(0, 4)
     def _(i):
-        rows = pl.ds(pl.multiple_of(i * 32, 32), 32)
-        h = hid[rows, :].astype(jnp.float32)
-        inv = lax.rsqrt(jnp.mean(h * h, axis=1, keepdims=True) + 1e-6)
-        xs[rows, :] = (h * inv * gain).astype(jnp.bfloat16)
+        get_hid(i).wait()
+
+        @pl.loop(0, quarter // 32)
+        def _(j):
+            rows = pl.ds(pl.multiple_of(i * quarter + j * 32, 32), 32)
+            h = hid[rows, :].astype(jnp.float32)
+            inv = lax.rsqrt(jnp.mean(h * h, axis=1, keepdims=True) + 1e-6)
+            xs[rows, :] = (h * inv * gain).astype(jnp.bfloat16)
 
     peak_s[...] = jnp.full(peak_s.shape, -jnp.inf, jnp.float32)
     sum_s[...] = jnp.zeros(sum_s.shape, jnp.float32)
@@ -403,7 +412,7 @@
                 pltpu.VMEM((chunks, CHUNK, width), f32), pltpu.VMEM((tokens, width), bf16),
                 pltpu.VMEM((8, width), f32), pltpu.VMEM((8, LANES), f32), pltpu.VMEM((8, LANES), f32),
                 pltpu.VMEM((n_tp, 2 * tokens // LANES, LANES), f32), pltpu.VMEM((n_tp, 16, LANES), f32),
-                dma((3,)), dma((vocab // BLOCK,)), dma((chunks,)), dma((chunks,)), dma(()),
+                dma((6,)), dma((vocab // BLOCK,)), dma((chunks,)), dma((chunks,)), dma(()),
                 dma((n_tp - 1,)), dma((n_tp - 1,)), dma((n_tp - 1,)), dma((n_tp - 1,)), dma((chunks, KINDS)), dma((chunks, KINDS)),
             ],
             compiler_params=pltpu.CompilerParams(collective_id=0, has_side_effects=True, vmem_limit_bytes=60 * 2**20),

time: 95.7 us -> 95.5 us (level)
  no operation moved by 1% of the time
where the time goes in v7:
time: 95.5 us; the launch traced here: 95.4 us
  Pallas kernels  81.7 us (86%)
  matrix products  10.5 us (11%)
  local copies, waits for them, and re-layouts  2.53 us (3%)
    pallas_call x1, Pallas kernels, local_step(): pl.pallas_call(functools.partial(kernel, n_tp), out_shape=(jax.ShapeDtype...  81.7 us
    dot_general x1, matrix products, local_step(): lax.dot_general(grad_z, x_in, (((0,), (0,)), ((), ())), preferred_element...  10.5 us

profile of v7, /device:TPU:81, one launch (start us, length us, event | category | flops | bytes accessed | tf_op | source)
XLA Modules:
  0.0 95.4 jit_solution(13408973788130932107)
XLA Ops:
  0.6 81.7 %shard_map.84 = (bf16[1024,1152]{1,0:T(8,128)(2,1)}, bf16[1024,1152]{1,0:T(8,128)(2,1)}, bf16[1024,2048]{1,0:T(8,128)(2,1)}, f32[16,128]{1,0:T(8,128)}) custom-call(bf16[1024,1152]{1,0:T(8,128)(2,1)} %hid_hbm.1, f32[1152]{0:T(1024)} %gain_ref.1, bf16[2048,1152]{1,0:T(8,128)(2,1)} %emb_hbm.1, s32[1024,256]{1,0:T(8,128)} %ids_hbm.1, f32[1024,256]{1,0:T(8,128)} %q_hbm.1), custom_call_target="tpu_custom_call" | custom-call | tf_op jit(solution)/shard_map/pallas_call | solution.py:401
  82.3 0.0 copy-start.1
  82.3 0.0 copy-start
  82.4 10.5 %fusion = f32[2048,1152]{1,0:T(8,128)} fusion(bf16[1024,2048]{1,0:T(8,128)(2,1)} %get-tuple-element.10, bf16[1024,1152]{1,0:T(8,128)(2,1)} %get-tuple-element.11), kind=kOutput, calls=%fused_computation.1 | convolution fusion | flops 4831838208 | bytes 15990784 | tf_op jit(solution)/shard_map/dot_general | solution.py:420
  92.9 0.0 copy-done.1
  92.9 0.6 slice_bitcast_fusion
  93.5 0.5 slice.6
  94.0 0.0 copy-done
  94.0 1.4 %copy.10 = bf16[1024,1152]{1,0:T(8,128)(2,1)} copy(bf16[1024,1152]{1,0:T(8,128)(2,1)S(1)} %copy-done) | data formatting | bytes 4718592
Async XLA Ops:
  82.3 10.6 %copy-start.1 = (f32[16,128]{1,0:T(8,128)S(1)}, f32[16,128]{1,0:T(8,128)}, u32[]{:S(2)}) copy-start(f32[16,128]{1,0:T(8,128)} %get-tuple-element.8) | copy-start | bytes 24580
  82.3 11.7 %copy-start = (bf16[1024,1152]{1,0:T(8,128)(2,1)S(1)}, bf16[1024,1152]{1,0:T(8,128)(2,1)}, u32[]{:S(2)}) copy-start(bf16[1024,1152]{1,0:T(8,128)(2,1)} %get-tuple-element.17) | copy-start | bytes 7077892
